TPU v7x, 8 devices: a whole 2x2x1 slice. The times are simulated.
8 devices in a mesh: dp: 1 (over z), col: 2 (over y), row: 4 (over x, core).
Axes of the slice: x: 2, y: 2, z: 1, core: 2. Of those that a mesh axis runs over, the one named last changes fastest.
Arguments:
- hidden: bfloat16 [64, 5120], P('dp', 'row')
- norm_gain: float32 [5120], P('row')
- w_head: bfloat16 [5120, 131072], P('row', 'col')
Outputs:
- output 1: float32 [64, 131072], P('dp', ('col', 'row'))
- output 2: float32 [64], P('dp')
All inputs are finite; a program needn't handle non-finite values.
Results may differ from a plain program's by a relative error of at most 0.001.
Values sent between devices are 32-bit elements.
A program may use at most 1 GiB of HBM per device.

v0:
```python
import jax
import jax.numpy as jnp
from jax import lax
from jax.sharding import PartitionSpec as P

EPS = 1e-5


def solution(mesh):
    row_count = mesh.shape["row"]

    def local_head(hidden, norm_gain, w_head):
        wide_hidden = hidden.astype(jnp.float32)
        local_sq = jnp.sum(wide_hidden * wide_hidden, axis=-1, keepdims=True)
        total_sq = lax.psum(local_sq, "row")
        mean_sq = total_sq / (hidden.shape[1] * row_count)
        normed = (wide_hidden * lax.rsqrt(mean_sq + EPS) * norm_gain).astype(jnp.bfloat16)
        share_logits = jnp.dot(normed, w_head, preferred_element_type=jnp.float32)
        logits = lax.psum_scatter(share_logits, "row", scatter_dimension=1, tiled=True)
        local_max = jnp.max(logits, axis=-1, keepdims=True)
        global_max = lax.pmax(local_max, ("col", "row"))
        local_mass = jnp.sum(jnp.exp(logits - global_max), axis=-1, keepdims=True)
        total_mass = lax.psum(local_mass, ("col", "row"))
        log_norm = global_max + jnp.log(total_mass)
        return logits - log_norm, log_norm[:, 0]

    return jax.shard_map(
        local_head,
        mesh=mesh,
        in_specs=(P("dp", "row"), P("row"), P("row", "col")),
        out_specs=(P("dp", ("col", "row")), P("dp")),
        check_vma=False,
    )
```

profile of v0, /device:TPU:0, one launch (start us, length us, event | category | flops | bytes accessed | tf_op | source)
XLA Modules:
  0.0 259.1 jit_solution(6844885644137076901)
XLA Ops:
  7.2 0.0 reduce-scatter.2.cloned.1.call-start
  7.2 1.0 fusion
  8.3 8.8 %psum.14 = f32[64,1]{0,1:T(1,128)S(1)} all-reduce(f32[64,1]{0,1:T(1,128)S(1)} %bitcast.12), channel_id=1, replica_groups=mesh['dp'=1,'col'=2,'row'=4] {'row'}, use_global_device_ids=true, to_apply=%region_1.0 | all-reduce | flops 64 | bytes 512 | tf_op jit(solution)/shard_map/psum | solution.py:15
  17.0 60.1 %fusion.3 = f32[64,65536]{1,0:T(8,128)} fusion(bf16[1280,65536]{1,0:T(8,128)(2,1)} %param.5, bf16[64,1280]{1,0:T(8,128)(2,1)} %param.3, f32[1280]{0:T(1024)} %param.4, f32[64]{0:T(128)S(1)} %rsqrt_bitcast_fusion), kind=kOutput, calls=%fused_computation.7 | convolution fusion | flops 10737745920 | bytes 184718592 | tf_op jit(solution)/shard_map/dot_general | solution.py:18
  77.1 0.0 reduce-scatter.2.cloned.1.call-update
  77.1 118.9 %reduce-scatter.2.cloned.1.call-done = f32[64,16384]{1,0:T(8,128)} async-done(((f32[64,65536]{1,0:T(8,128)}), f32[64,16384]{1,0:T(8,128)}) %reduce-scatter.2.cloned.1.call-update) | async-done | bytes 4194320 | tf_op jit(solution)/shard_map/reduce_scatter | solution.py:19
  196.1 2.5 reduce_max.9
  198.5 22.2 %pmax.7 = f32[64,1]{0,1:T(1,128)S(1)} all-reduce(f32[64,1]{0,1:T(1,128)S(1)} %bitcast.11), channel_id=1, replica_groups=mesh['dp'=1,'col'=2,'row'=4] {'col','row'}, use_global_device_ids=true, to_apply=%region_4.0 | all-reduce | flops 64 | bytes 512 | tf_op jit(solution)/shard_map/pmax | solution.py:21
  220.8 2.9 %exponential_reduce_fusion = f32[64]{0:T(128)S(1)} fusion(f32[64,16384]{1,0:T(8,128)} %reduce-scatter.2.cloned.1.call-done, f32[64]{0:T(128)S(1)} %bitcast.10), kind=kLoop, calls=%fused_computation | loop fusion | flops 2097088 | bytes 4194816 | tf_op jit(solution)/shard_map/reduce_sum | solution.py:22
  223.7 24.0 %psum.15 = f32[64,1]{0,1:T(1,128)S(1)} all-reduce(f32[64,1]{0,1:T(1,128)S(1)} %bitcast.13), channel_id=1, replica_groups=mesh['dp'=1,'col'=2,'row'=4] {'col','row'}, use_global_device_ids=true, to_apply=%region_6.0 | all-reduce | flops 64 | bytes 512 | tf_op jit(solution)/shard_map/psum | solution.py:23
  247.7 0.0 copy-start
  247.7 4.6 %broadcast_subtract_fusion = f32[64,16384]{1,0:T(8,128)} fusion(f32[64,16384]{1,0:T(8,128)} %reduce-scatter.2.cloned.1.call-done, f32[64]{0:T(128)S(1)} %add_bitcast_fusion), kind=kLoop, calls=%fused_computation.1 | loop fusion | flops 1048576 | bytes 8388864 | tf_op jit(solution)/shard_map/sub | solution.py:25
  252.3 0.0 copy-done
  (2 shorter events, 0.0 us)
Async XLA Ops:
  7.2 188.9 %reduce-scatter.2.cloned.1.call-start = ((), (), s32[]{:S(2)}) async-start(), calls=%async_computation.1 | async-start | bytes 20971520 | tf_op jit(solution)/shard_map/reduce_scatter | solution.py:19
  247.7 4.6 %copy-start = (f32[64]{0:T(128)}, f32[64]{0:T(128)S(1)}, u32[]{:S(2)}) copy-start(f32[64]{0:T(128)S(1)} %add_bitcast_fusion) | copy-start | bytes 772
Sparse Core Ops, SparseCore 0:
  77.2 118.7 reduce-scatter.1
where the time goes:
time: 260 us; the launch traced here: 259 us
  waiting for transfers between devices  119 us (46%)
  matrix products  60.1 us (23%)
  blocking collectives  55 us (21%)
  between operations  14 us (5%)
  other arithmetic  11 us (4%)
    reduce_scatter x1, waiting for transfers between devices, local_head(): lax.psum_scatter(share_logits, 'row', scatter_dimension=1, tiled=True)  119 us
    dot_general x1, matrix products, local_head(): share_logits = jnp.dot(normed, w_head, preferred_element_type=jnp.float32)  60.1 us
    psum x1, blocking collectives, local_head(): total_mass = lax.psum(local_mass, ('col', 'row'))  24 us
    pmax x1, blocking collectives, local_head(): global_max = lax.pmax(local_max, ('col', 'row'))  22.2 us
    psum x1, blocking collectives, local_head(): total_sq = lax.psum(local_sq, 'row')  8.75 us
  transfers between devices with their start and end apart: 1, of which 1 were waited for; matrix products, arithmetic and copies ran while one was open for 0% of the time, Pallas kernels for 0%

commit v1 on v0

v1 whole, which is shorter than its diff:
```python
import functools

import jax
import jax.numpy as jnp
from jax import lax
from jax.experimental import pallas as pl
from jax.experimental.pallas import tpu as pltpu
from jax.sharding import PartitionSpec as P

EPS = 1e-5
MESH = pl.DeviceIdType.MESH
LANES = 128
TILE = 512
PAIRS = 6
VMEM_LIMIT = 56 * 1024 * 1024


def head_kernel(
    sizes,
    hidden_hbm,
    gain_ref,
    w_hbm,
    z_ref,
    lse_col_ref,
    lse_row_ref,
    h_ref,
    x_ref,
    w_own,
    w_partner,
    core_out,
    core_in,
    chip_out,
    chip_in,
    sq_out,
    sq_in,
    mass_out,
    mass_in,
    h_sem,
    w_own_sem,
    w_partner_sem,
    core_send,
    core_recv,
    chip_send,
    chip_recv,
    sq_send,
    sq_recv,
    mass_send,
    mass_recv,
):
    cols, rows, width, block, tiles, features = sizes
    dp, col, row = lax.axis_index("dp"), lax.axis_index("col"), lax.axis_index("row")
    chip, core = row // 2, row % 2
    me = col * rows + row
    partner = (dp, col, chip * 2 + 1 - core)
    across = (dp, col, (1 - chip) * 2 + core)
    batch = h_ref.shape[0]

    def w_copy(q, own):
        phase = q // tiles
        target_chip = phase * chip + (1 - phase) * (1 - chip)
        target_core = core if own else 1 - core
        start = (target_chip * 2 + target_core) * block + (q % tiles) * TILE
        buf, sem = (w_own, w_own_sem) if own else (w_partner, w_partner_sem)
        slot = q % PAIRS
        return pltpu.make_async_copy(
            w_hbm.at[:, pl.ds(pl.multiple_of(start, TILE), TILE)], buf.at[slot], sem.at[slot]
        )

    def core_copy(q):
        return pltpu.make_async_remote_copy(
            core_out.at[q], core_in.at[q], core_send.at[q], core_recv.at[q],
            device_id=partner, device_id_type=MESH,
        )

    def chip_copy(i):
        return pltpu.make_async_remote_copy(
            chip_out.at[i], chip_in.at[i], chip_send.at[i], chip_recv.at[i],
            device_id=across, device_id_type=MESH,
        )

    h_copy = pltpu.make_async_copy(hidden_hbm, h_ref, h_sem)
    h_copy.start()
    w_copy(0, False).start()
    w_copy(0, True).start()

    barrier = pltpu.get_barrier_semaphore()
    everyone = cols * rows
    peers = []
    for k in range(1, everyone):
        d = (me + k) % everyone
        peers.append((dp, d // rows, d % rows))
    for peer in peers:
        pl.semaphore_signal(barrier, inc=1, device_id=peer, device_id_type=MESH)

    @pl.loop(1, PAIRS)
    def _(q):
        w_copy(q, False).start()
        w_copy(q, True).start()

    h_copy.wait()
    squares = jnp.zeros((batch, LANES), jnp.float32)
    for k in range(width // LANES):
        part = h_ref[:, k * LANES:(k + 1) * LANES].astype(jnp.float32)
        squares = squares + part * part
    local_sq = jnp.sum(jnp.concatenate([squares, squares], axis=0).T, axis=0, keepdims=True)
    sq_out[...] = local_sq
    sq_in[row] = local_sq
    pl.semaphore_wait(barrier, everyone - 1)

    def sq_copy(k):
        other = (row + k) % rows
        return pltpu.make_async_remote_copy(
            sq_out, sq_in.at[row], sq_send.at[k], sq_recv.at[row],
            device_id=(dp, col, other), device_id_type=MESH,
        )

    def sq_arrival(k):
        other = (row + k) % rows
        return pltpu.make_async_remote_copy(
            sq_out, sq_in.at[other], sq_send.at[k], sq_recv.at[other],
            device_id=(dp, col, other), device_id_type=MESH,
        )

    for k in range(1, rows):
        sq_copy(k).start()
    for k in range(1, rows):
        sq_arrival(k).wait_recv()
    total_sq = sq_in[0]
    for k in range(1, rows):
        total_sq = total_sq + sq_in[k]
    scale_row = lax.rsqrt(total_sq / features + EPS)
    scale = jnp.broadcast_to(scale_row, (LANES, LANES)).T[:batch]
    for k in range(width // LANES):
        at = slice(k * LANES, (k + 1) * LANES)
        x_ref[:, at] = (h_ref[:, at].astype(jnp.float32) * scale * gain_ref[:, at]).astype(jnp.bfloat16)

    def partner_tile(q):
        w_copy(q, False).wait()
        core_out[q] = jnp.dot(x_ref[...], w_partner[q % PAIRS], preferred_element_type=jnp.float32)

        @pl.when(q + PAIRS < 2 * tiles)
        def _():
            w_copy(q + PAIRS, False).start()

        core_copy(q).start()

    def own_tile(q):
        w_copy(q, True).wait()
        share = jnp.dot(x_ref[...], w_own[q % PAIRS], preferred_element_type=jnp.float32)

        @pl.when(q + PAIRS < 2 * tiles)
        def _():
            w_copy(q + PAIRS, True).start()

        core_copy(q).wait_recv()
        return share + core_in[q]

    def columns(i):
        return pl.ds(pl.multiple_of(i * TILE, TILE), TILE)

    partner_tile(0)

    @pl.loop(0, tiles)
    def _(q):
        partner_tile(q + 1)
        chip_out[q] = own_tile(q)
        chip_copy(q).start()

    @pl.loop(0, tiles - 1)
    def _(i):
        partner_tile(tiles + i + 1)
        z_ref[:, columns(i)] = own_tile(tiles + i)

    z_ref[:, (tiles - 1) * TILE:] = own_tile(2 * tiles - 1)

    def finish(i, carry):
        peak, mass = carry
        chip_copy(i).wait_recv()
        z = z_ref[:, columns(i)] + chip_in[i]
        z_ref[:, columns(i)] = z
        parts = [z[:, k * LANES:(k + 1) * LANES] for k in range(TILE // LANES)]
        new_peak = functools.reduce(jnp.maximum, parts, peak)
        mass = mass * jnp.exp(peak - new_peak)
        for part in parts:
            mass = mass + jnp.exp(part - new_peak)
        return new_peak, mass

    start = (jnp.full((batch, LANES), -jnp.inf, jnp.float32), jnp.zeros((batch, LANES), jnp.float32))
    lane_peak, lane_mass = lax.fori_loop(0, tiles, finish, start)
    peak = jnp.max(lane_peak, axis=1, keepdims=True)
    mass = jnp.sum(lane_mass * jnp.exp(lane_peak - peak), axis=1, keepdims=True)
    lane = lax.broadcasted_iota(jnp.int32, (batch, LANES), 1)
    pair = jnp.where(lane == 0, peak, mass)
    message = jnp.concatenate([pair, pair], axis=0).T[:8]
    mass_out[...] = message
    mass_in[me] = message

    for k in range(1, everyone):
        pltpu.make_async_remote_copy(
            mass_out, mass_in.at[me], mass_send.at[k], mass_recv.at[me],
            device_id=peers[k - 1], device_id_type=MESH,
        ).start()
    for k in range(1, everyone):
        other = (me + k) % everyone
        pltpu.make_async_remote_copy(
            mass_out, mass_in.at[other], mass_send.at[k], mass_recv.at[other],
            device_id=peers[k - 1], device_id_type=MESH,
        ).wait_recv()
    peaks = [mass_in[d, 0:1] for d in range(everyone)]
    top = functools.reduce(jnp.maximum, peaks)
    total = jnp.zeros_like(top)
    for d in range(everyone):
        total = total + mass_in[d, 1:2] * jnp.exp(peaks[d] - top)
    log_norm = top + jnp.log(total)
    lse_row_ref[...] = log_norm
    lse_col_ref[...] = jnp.broadcast_to(log_norm, (LANES, LANES)).T[:batch]

    for k in range(1, rows):
        sq_copy(k).wait_send()
    for k in range(1, everyone):
        pltpu.make_async_remote_copy(
            mass_out, mass_in.at[me], mass_send.at[k], mass_recv.at[me],
            device_id=peers[k - 1], device_id_type=MESH,
        ).wait_send()

    @pl.loop(0, tiles)
    def _(i):
        core_copy(i).wait_send()
        core_copy(tiles + i).wait_send()
        chip_copy(i).wait_send()


def solution(mesh):
    cols, rows = mesh.shape["col"], mesh.shape["row"]

    def local_head(hidden, norm_gain, w_head):
        batch, width = hidden.shape
        block = w_head.shape[1] // rows
        tiles = block // TILE
        sizes = (cols, rows, width, block, tiles, width * rows)
        f32 = jnp.float32
        dma = pltpu.SemaphoreType.DMA
        z, lse_col, lse_row = pl.pallas_call(
            functools.partial(head_kernel, sizes),
            name="head",
            out_shape=(
                jax.ShapeDtypeStruct((batch, block), f32),
                jax.ShapeDtypeStruct((batch, LANES), f32),
                jax.ShapeDtypeStruct((1, LANES), f32),
            ),
            in_specs=[
                pl.BlockSpec(memory_space=pl.ANY),
                pl.BlockSpec(memory_space=pltpu.VMEM),
                pl.BlockSpec(memory_space=pl.ANY),
            ],
            out_specs=[pl.BlockSpec(memory_space=pltpu.VMEM)] * 3,
            scratch_shapes=[
                pltpu.VMEM((batch, width), jnp.bfloat16),
                pltpu.VMEM((batch, width), jnp.bfloat16),
                pltpu.VMEM((PAIRS, width, TILE), jnp.bfloat16),
                pltpu.VMEM((PAIRS, width, TILE), jnp.bfloat16),
                pltpu.VMEM((2 * tiles, batch, TILE), f32),
                pltpu.VMEM((2 * tiles, batch, TILE), f32),
                pltpu.VMEM((tiles, batch, TILE), f32),
                pltpu.VMEM((tiles, batch, TILE), f32),
                pltpu.VMEM((1, LANES), f32),
                pltpu.VMEM((rows, 1, LANES), f32),
                pltpu.VMEM((8, LANES), f32),
                pltpu.VMEM((cols * rows, 8, LANES), f32),
                dma,
                dma((PAIRS,)),
                dma((PAIRS,)),
                dma((2 * tiles,)),
                dma((2 * tiles,)),
                dma((tiles,)),
                dma((tiles,)),
                dma((rows,)),
                dma((rows,)),
                dma((cols * rows,)),
                dma((cols * rows,)),
            ],
            compiler_params=pltpu.CompilerParams(
                collective_id=0, has_side_effects=True, vmem_limit_bytes=VMEM_LIMIT
            ),
        )(hidden, norm_gain.reshape(1, width), w_head)
        return z - lse_col[:, :1], lse_row[0, :batch]

    return jax.shard_map(
        local_head,
        mesh=mesh,
        in_specs=(P("dp", "row"), P("row"), P("row", "col")),
        out_specs=(P("dp", ("col", "row")), P("dp")),
        check_vma=False,
    )
```

time: 260 us -> 117 us (0.45)
  waiting for transfers between devices: 119 us -> 0 us
  Pallas kernels: 0 us -> 109 us
  matrix products: 60.1 us -> 0 us
  blocking collectives: 55 us -> 0 us
  between operations: 14 us -> 0.65 us
  other arithmetic: 11 us -> 4.59 us
  local copies, waits for them, and re-layouts: 0.01 us -> 2.67 us
    reduce_scatter x1 -> x0, waiting for transfers between devices: 119 us -> none  [local_head(): lax.psum_scatter(share_logits, 'row', scatter_dimension=1, tiled=True)]
    pallas_call x0 -> x1, Pallas kernels: none -> 109 us  [local_head(): pl.pallas_call(functools.partial(head_kernel, sizes), name='head', out_sh...]
    dot_general x1 -> x0, matrix products: 60.1 us -> none  [local_head(): share_logits = jnp.dot(normed, w_head, preferred_element_type=jnp.float32)]
    psum x2 -> x0, blocking collectives: 32.7 us -> none  [the longest x1 24 us: local_head(): total_mass = lax.psum(local_mass, ('col', 'row'))]
    pmax x1 -> x0, blocking collectives: 22.2 us -> none  [local_head(): global_max = lax.pmax(local_max, ('col', 'row'))]
    reduce_sum x2 -> x0, other arithmetic: 3.95 us -> none  [the longest x1 2.9 us: local_head(): local_mass = jnp.sum(jnp.exp(logits - global_max), axis=-1, keepdims=True)]
  transfers between devices with their start and end apart: 1 -> 0, of which waited for: 1 -> 0; matrix products, arithmetic and copies ran while one was open for 0% -> 0% of each run, Pallas kernels for 0% -> 0%
where the time goes in v1:
time: 117 us
  Pallas kernels  109 us (93%)
  other arithmetic  4.59 us (4%)
  local copies, waits for them, and re-layouts  2.67 us (2%)
    pallas_call x1, Pallas kernels, local_head(): pl.pallas_call(functools.partial(head_kernel, sizes), name='head', out_sh...  109 us
    sub x1, other arithmetic, local_head(): return (z - lse_col[:, :1], lse_row[0, :batch])  4.59 us

profile of v1, /device:TPU:0, one launch (start us, length us, event | category | flops | bytes accessed | tf_op | source)
XLA Modules:
  0.0 116.6 jit_solution(14319421208468657159)
XLA Ops:
  0.6 1.3 %reshape.7.gain_ref = f32[1,1280]{1,0:T(1,128)} reshape(f32[1280]{0:T(1024)} %param.4) | data formatting | bytes 10240 | tf_op jit(solution)/shard_map/reshape | solution.py:285
  1.9 108.7 %head.1 = (f32[64,16384]{1,0:T(8,128)}, f32[64,128]{1,0:T(8,128)}, f32[1,128]{1,0:T(1,128)}) custom-call(bf16[64,1280]{1,0:T(8,128)(2,1)} %hidden_hbm.1, f32[1,1280]{1,0:T(1,128)} %reshape.7.gain_ref, bf16[1280,65536]{1,0:T(8,128)(2,1)} %w_hbm.1), custom_call_target="tpu_custom_call" | custom-call | tf_op jit(solution)/shard_map/head/pallas_call | solution.py:243
  110.7 0.9 slice_reduce_fusion
  111.5 0.0 copy-start
  111.5 4.6 %broadcast_subtract_fusion = f32[64,16384]{1,0:T(8,128)} fusion(f32[64,16384]{1,0:T(8,128)} %get-tuple-element.5, f32[64]{0:T(128)S(1)} %slice_reduce_fusion), kind=kLoop, calls=%fused_computation | loop fusion | flops 1048576 | bytes 8388864 | tf_op jit(solution)/shard_map/sub | solution.py:286
  116.1 0.0 copy-done
  116.1 0.5 slice_bitcast_fusion
Async XLA Ops:
  111.5 4.6 %copy-start = (f32[1,128]{1,0:T(1,128)S(1)}, f32[1,128]{1,0:T(1,128)}, u32[]{:S(2)}) copy-start(f32[1,128]{1,0:T(1,128)} %get-tuple-element.7) | copy-start | bytes 1540

commit v2 on v1

--- a/solution.py
+++ b/solution.py
@@ -12,18 +12,20 @@
 LANES = 128
 TILE = 512
 PAIRS = 6
-VMEM_LIMIT = 56 * 1024 * 1024
+CHUNKS = 8
+VMEM_LIMIT = 48 * 1024 * 1024
 
 
 def head_kernel(
     sizes,
     hidden_hbm,
-    gain_ref,
+    gain_hbm,
     w_hbm,
     z_ref,
     lse_col_ref,
     lse_row_ref,
     h_ref,
+    gain_ref,
     x_ref,
     w_own,
     w_partner,
@@ -36,6 +38,7 @@
     mass_out,
     mass_in,
     h_sem,
+    gain_sem,
     w_own_sem,
     w_partner_sem,
     core_send,
@@ -79,7 +82,9 @@
         )
 
     h_copy = pltpu.make_async_copy(hidden_hbm, h_ref, h_sem)
+    gain_copy = pltpu.make_async_copy(gain_hbm, gain_ref, gain_sem)
     h_copy.start()
+    gain_copy.start()
     w_copy(0, False).start()
     w_copy(0, True).start()
 
@@ -98,6 +103,7 @@
         w_copy(q, True).start()
 
     h_copy.wait()
+    gain_copy.wait()
     squares = jnp.zeros((batch, LANES), jnp.float32)
     for k in range(width // LANES):
         part = h_ref[:, k * LANES:(k + 1) * LANES].astype(jnp.float32)
@@ -132,7 +138,7 @@
     scale = jnp.broadcast_to(scale_row, (LANES, LANES)).T[:batch]
     for k in range(width // LANES):
         at = slice(k * LANES, (k + 1) * LANES)
-        x_ref[:, at] = (h_ref[:, at].astype(jnp.float32) * scale * gain_ref[:, at]).astype(jnp.bfloat16)
+        x_ref[:, at] = (h_ref[:, at].astype(jnp.float32) * scale * gain_ref[at]).astype(jnp.bfloat16)
 
     def partner_tile(q):
         w_copy(q, False).wait()
@@ -230,6 +236,21 @@
         chip_copy(i).wait_send()
 
 
+def subtract_kernel(z_ref, lse_col_ref, lse_row_ref, out_hbm, log_norm_ref, out_ref, sem):
+    batch, block = z_ref.shape
+    lse = lse_col_ref[...]
+    copies = []
+    for n in range(CHUNKS):
+        for k in range(n * block // CHUNKS, (n + 1) * block // CHUNKS, LANES):
+            out_ref[:, k:k + LANES] = z_ref[:, k:k + LANES] - lse
+        at = pl.ds(n * block // CHUNKS, block // CHUNKS)
+        copies.append(pltpu.make_async_copy(out_ref.at[:, at], out_hbm.at[:, at], sem.at[n]))
+        copies[-1].start()
+    log_norm_ref[...] = lse_row_ref[0, :batch]
+    for copy in copies:
+        copy.wait()
+
+
 def solution(mesh):
     cols, rows = mesh.shape["col"], mesh.shape["row"]
 
@@ -240,22 +261,21 @@
         sizes = (cols, rows, width, block, tiles, width * rows)
         f32 = jnp.float32
         dma = pltpu.SemaphoreType.DMA
+        vmem = pl.BlockSpec(memory_space=pltpu.VMEM)
+        hbm = pl.BlockSpec(memory_space=pl.ANY)
         z, lse_col, lse_row = pl.pallas_call(
             functools.partial(head_kernel, sizes),
             name="head",
             out_shape=(
-                jax.ShapeDtypeStruct((batch, block), f32),
-                jax.ShapeDtypeStruct((batch, LANES), f32),
-                jax.ShapeDtypeStruct((1, LANES), f32),
+                pltpu.VMEM((batch, block), f32),
+                pltpu.VMEM((batch, LANES), f32),
+                pltpu.VMEM((1, LANES), f32),
             ),
-            in_specs=[
-                pl.BlockSpec(memory_space=pl.ANY),
-                pl.BlockSpec(memory_space=pltpu.VMEM),
-                pl.BlockSpec(memory_space=pl.ANY),
-            ],
-            out_specs=[pl.BlockSpec(memory_space=pltpu.VMEM)] * 3,
+            in_specs=[pl.BlockSpec(memory_space=pltpu.HBM)] * 3,
+            out_specs=[vmem] * 3,
             scratch_shapes=[
                 pltpu.VMEM((batch, width), jnp.bfloat16),
+                pltpu.VMEM((width,), f32),
                 pltpu.VMEM((batch, width), jnp.bfloat16),
                 pltpu.VMEM((PAIRS, width, TILE), jnp.bfloat16),
                 pltpu.VMEM((PAIRS, width, TILE), jnp.bfloat16),
@@ -267,6 +287,7 @@
                 pltpu.VMEM((rows, 1, LANES), f32),
                 pltpu.VMEM((8, LANES), f32),
                 pltpu.VMEM((cols * rows, 8, LANES), f32),
+                dma,
                 dma,
                 dma((PAIRS,)),
                 dma((PAIRS,)),
@@ -282,8 +303,19 @@
             compiler_params=pltpu.CompilerParams(
                 collective_id=0, has_side_effects=True, vmem_limit_bytes=VMEM_LIMIT
             ),
-        )(hidden, norm_gain.reshape(1, width), w_head)
-        return z - lse_col[:, :1], lse_row[0, :batch]
+        )(*(pltpu.with_memory_space_constraint(a, pltpu.HBM) for a in (hidden, norm_gain, w_head)))
+        return pl.pallas_call(
+            subtract_kernel,
+            name="subtract",
+            out_shape=(
+                jax.ShapeDtypeStruct((batch, block), f32),
+                jax.ShapeDtypeStruct((batch,), f32),
+            ),
+            in_specs=[vmem] * 3,
+            out_specs=[hbm, vmem],
+            scratch_shapes=[pltpu.VMEM((batch, block), f32), dma((CHUNKS,))],
+            compiler_params=pltpu.CompilerParams(vmem_limit_bytes=16 * 1024 * 1024),
+        )(z, lse_col, lse_row)
 
     return jax.shard_map(
         local_head,

time: 117 us -> 109 us (0.932)
  other arithmetic: 4.59 us -> 0 us
  local copies, waits for them, and re-layouts: 2.67 us -> 0 us
    sub x1 -> x0, other arithmetic: 4.59 us -> none  [local_head(): return (z - lse_col[:, :1], lse_row[0, :batch])]
    pallas_call x1, Pallas kernels: 109 us -> 106 us  [local_head(): pl.pallas_call(functools.partial(head_kernel, sizes), name='head', out_sh...]
    pallas_call x0 -> x1, Pallas kernels: none -> 2.62 us  [local_head(): pl.pallas_call(subtract_kernel, name='subtract', out_shape=(jax.ShapeDtyp...]
    reshape x1 -> x0, local copies, waits for them, and re-layouts: 1.29 us -> none  [local_head(): norm_gain.reshape(1, width)]
where the time goes in v2:
time: 109 us
  Pallas kernels  109 us (100%)
    pallas_call x1, Pallas kernels, local_head(): pl.pallas_call(functools.partial(head_kernel, sizes), name='head', out_sh...  106 us
    pallas_call x1, Pallas kernels, local_head(): pl.pallas_call(subtract_kernel, name='subtract', out_shape=(jax.ShapeDtyp...  2.62 us

profile of v2, /device:TPU:0, one launch (start us, length us, event | category | flops | bytes accessed | tf_op | source)
XLA Modules:
  0.0 109.4 jit_solution(10046550785194640927)
XLA Ops:
  0.6 106.1 %head.1 = (f32[64,16384]{1,0:T(8,128)S(1)}, f32[64,128]{1,0:T(8,128)S(1)}, f32[1,128]{1,0:T(1,128)S(1)}) custom-call(bf16[64,1280]{1,0:T(8,128)(2,1)} %hidden_hbm.1, f32[1280]{0:T(1024)} %gain_hbm.1, bf16[1280,65536]{1,0:T(8,128)(2,1)} %w_hbm.1), custom_call_target="tpu_custom_call" | custom-call | tf_op jit(solution)/shard_map/head/pallas_call | solution.py:266
  106.7 2.6 %subtract.1 = (f32[64,16384]{1,0:T(8,128)}, f32[64]{0:T(128)}) custom-call(f32[64,16384]{1,0:T(8,128)S(1)} %get-tuple-element.5.z_ref, f32[64,128]{1,0:T(8,128)S(1)} %get-tuple-element.6.lse_col_ref, f32[1,128]{1,0:T(1,128)S(1)} %get-tuple-element.7.lse_row_ref), custom_call_target="tpu_custom_call" | custom-call | tf_op jit(solution)/shard_map/subtract/pallas_call | solution.py:307

commit v3 on v2

--- a/solution.py
+++ b/solution.py
@@ -85,8 +85,6 @@
     gain_copy = pltpu.make_async_copy(gain_hbm, gain_ref, gain_sem)
     h_copy.start()
     gain_copy.start()
-    w_copy(0, False).start()
-    w_copy(0, True).start()
 
     barrier = pltpu.get_barrier_semaphore()
     everyone = cols * rows
@@ -97,7 +95,7 @@
     for peer in peers:
         pl.semaphore_signal(barrier, inc=1, device_id=peer, device_id_type=MESH)
 
-    @pl.loop(1, PAIRS)
+    @pl.loop(0, PAIRS)
     def _(q):
         w_copy(q, False).start()
         w_copy(q, True).start()
@@ -150,16 +148,16 @@
 
         core_copy(q).start()
 
-    def own_tile(q):
+    def own_tile(q, total):
         w_copy(q, True).wait()
-        share = jnp.dot(x_ref[...], w_own[q % PAIRS], preferred_element_type=jnp.float32)
+        total[...] = jnp.dot(x_ref[...], w_own[q % PAIRS], preferred_element_type=jnp.float32)
 
         @pl.when(q + PAIRS < 2 * tiles)
         def _():
             w_copy(q + PAIRS, True).start()
 
         core_copy(q).wait_recv()
-        return share + core_in[q]
+        total[...] += core_in[q]
 
     def columns(i):
         return pl.ds(pl.multiple_of(i * TILE, TILE), TILE)
@@ -169,15 +167,15 @@
     @pl.loop(0, tiles)
     def _(q):
         partner_tile(q + 1)
-        chip_out[q] = own_tile(q)
+        own_tile(q, chip_out.at[q])
         chip_copy(q).start()
 
     @pl.loop(0, tiles - 1)
     def _(i):
         partner_tile(tiles + i + 1)
-        z_ref[:, columns(i)] = own_tile(tiles + i)
-
-    z_ref[:, (tiles - 1) * TILE:] = own_tile(2 * tiles - 1)
+        own_tile(tiles + i, z_ref.at[:, columns(i)])
+
+    own_tile(2 * tiles - 1, z_ref.at[:, (tiles - 1) * TILE:])
 
     def finish(i, carry):
         peak, mass = carry

time: 109 us -> 109 us (level)
  no operation moved by 1% of the time
where the time goes in v3:
time: 109 us
  Pallas kernels  108 us (99%)
    pallas_call x1, Pallas kernels, local_head(): pl.pallas_call(functools.partial(head_kernel, sizes), name='head', out_sh...  106 us
    pallas_call x1, Pallas kernels, local_head(): pl.pallas_call(subtract_kernel, name='subtract', out_shape=(jax.ShapeDtyp...  2.62 us

profile of v3, /device:TPU:0, one launch (start us, length us, event | category | flops | bytes accessed | tf_op | source)
XLA Modules:
  0.0 109.0 jit_solution(10710396016163816189)
XLA Ops:
  0.6 105.8 %head.1 = (f32[64,16384]{1,0:T(8,128)S(1)}, f32[64,128]{1,0:T(8,128)S(1)}, f32[1,128]{1,0:T(1,128)S(1)}) custom-call(bf16[64,1280]{1,0:T(8,128)(2,1)} %hidden_hbm.1, f32[1280]{0:T(1024)} %gain_hbm.1, bf16[1280,65536]{1,0:T(8,128)(2,1)} %w_hbm.1), custom_call_target="tpu_custom_call" | custom-call | tf_op jit(solution)/shard_map/head/pallas_call | solution.py:264
  106.4 2.6 %subtract.1 = (f32[64,16384]{1,0:T(8,128)}, f32[64]{0:T(128)}) custom-call(f32[64,16384]{1,0:T(8,128)S(1)} %get-tuple-element.5.z_ref, f32[64,128]{1,0:T(8,128)S(1)} %get-tuple-element.6.lse_col_ref, f32[1,128]{1,0:T(1,128)S(1)} %get-tuple-element.7.lse_row_ref), custom_call_target="tpu_custom_call" | custom-call | tf_op jit(solution)/shard_map/subtract/pallas_call | solution.py:305

commit v4 on v3

--- a/solution.py
+++ b/solution.py
@@ -12,6 +12,7 @@
 LANES = 128
 TILE = 512
 PAIRS = 6
+SHIFT = 1
 CHUNKS = 8
 VMEM_LIMIT = 48 * 1024 * 1024
 
@@ -53,32 +54,51 @@
     cols, rows, width, block, tiles, features = sizes
     dp, col, row = lax.axis_index("dp"), lax.axis_index("col"), lax.axis_index("row")
     chip, core = row // 2, row % 2
-    me = col * rows + row
-    partner = (dp, col, chip * 2 + 1 - core)
-    across = (dp, col, (1 - chip) * 2 + core)
     batch = h_ref.shape[0]
 
-    def w_copy(q, own):
-        phase = q // tiles
-        target_chip = phase * chip + (1 - phase) * (1 - chip)
-        target_core = core if own else 1 - core
-        start = (target_chip * 2 + target_core) * block + (q % tiles) * TILE
+    def device(flip_col, flip_chip, flip_core):
+        c = 1 - col if flip_col else col
+        r = (1 - chip if flip_chip else chip) * 2 + (1 - core if flip_core else core)
+        return (dp, c, r), c * rows + r
+
+    me = device(0, 0, 0)[1]
+    row_peers = [device(0, 1, 1), device(0, 1, 0), device(0, 0, 1)]
+    mirror = device(1, 0, 0)
+    peers = [device(1, 1, 1), device(1, 1, 0), device(1, 0, 1), mirror, *row_peers]
+    partner = row_peers[2][0]
+
+    own_count = tiles - SHIFT + core * 2 * SHIFT
+    partner_count = 2 * tiles - own_count
+
+    def w_copy(s, own):
+        count = own_count if own else partner_count
+        side = core if own else 1 - core
+        late = jnp.where(s < count, 0, 1)
+        tile = (1 - late) * (side * (tiles - SHIFT) + s) + late * (side * tiles + s - count)
+        start = (late * chip + (1 - late) * (1 - chip)) * 2 * block + tile * TILE
         buf, sem = (w_own, w_own_sem) if own else (w_partner, w_partner_sem)
-        slot = q % PAIRS
+        slot = s % PAIRS
         return pltpu.make_async_copy(
             w_hbm.at[:, pl.ds(pl.multiple_of(start, TILE), TILE)], buf.at[slot], sem.at[slot]
         )
 
-    def core_copy(q):
-        return pltpu.make_async_remote_copy(
-            core_out.at[q], core_in.at[q], core_send.at[q], core_recv.at[q],
+    def core_copy(s):
+        return pltpu.make_async_remote_copy(
+            core_out.at[s], core_in.at[s], core_send.at[s], core_recv.at[s],
             device_id=partner, device_id_type=MESH,
         )
 
-    def chip_copy(i):
-        return pltpu.make_async_remote_copy(
-            chip_out.at[i], chip_in.at[i], chip_send.at[i], chip_recv.at[i],
-            device_id=across, device_id_type=MESH,
+    def chip_copy(s):
+        tile = core * (tiles - SHIFT) + s
+        return pltpu.make_async_remote_copy(
+            chip_out.at[s], chip_in.at[tile % tiles], chip_send.at[s], chip_recv.at[tile % tiles],
+            device_id=(dp, col, (1 - chip) * 2 + tile // tiles), device_id_type=MESH,
+        )
+
+    def chip_arrival(i):
+        return pltpu.make_async_remote_copy(
+            chip_out.at[0], chip_in.at[i], chip_send.at[0], chip_recv.at[i],
+            device_id=row_peers[1][0], device_id_type=MESH,
         )
 
     h_copy = pltpu.make_async_copy(hidden_hbm, h_ref, h_sem)
@@ -87,12 +107,7 @@
     gain_copy.start()
 
     barrier = pltpu.get_barrier_semaphore()
-    everyone = cols * rows
-    peers = []
-    for k in range(1, everyone):
-        d = (me + k) % everyone
-        peers.append((dp, d // rows, d % rows))
-    for peer in peers:
+    for peer, _ in [mirror, *row_peers]:
         pl.semaphore_signal(barrier, inc=1, device_id=peer, device_id_type=MESH)
 
     @pl.loop(0, PAIRS)
@@ -109,26 +124,20 @@
     local_sq = jnp.sum(jnp.concatenate([squares, squares], axis=0).T, axis=0, keepdims=True)
     sq_out[...] = local_sq
     sq_in[row] = local_sq
-    pl.semaphore_wait(barrier, everyone - 1)
-
-    def sq_copy(k):
-        other = (row + k) % rows
-        return pltpu.make_async_remote_copy(
-            sq_out, sq_in.at[row], sq_send.at[k], sq_recv.at[row],
-            device_id=(dp, col, other), device_id_type=MESH,
-        )
-
-    def sq_arrival(k):
-        other = (row + k) % rows
-        return pltpu.make_async_remote_copy(
-            sq_out, sq_in.at[other], sq_send.at[k], sq_recv.at[other],
-            device_id=(dp, col, other), device_id_type=MESH,
-        )
-
-    for k in range(1, rows):
+    pl.semaphore_wait(barrier, rows)
+
+    def sq_copy(k, arrival=False):
+        peer, _ = row_peers[k]
+        slot = peer[2] if arrival else row
+        return pltpu.make_async_remote_copy(
+            sq_out, sq_in.at[slot], sq_send.at[k], sq_recv.at[slot],
+            device_id=peer, device_id_type=MESH,
+        )
+
+    for k in range(rows - 1):
         sq_copy(k).start()
-    for k in range(1, rows):
-        sq_arrival(k).wait_recv()
+    for k in reversed(range(rows - 1)):
+        sq_copy(k, arrival=True).wait_recv()
     total_sq = sq_in[0]
     for k in range(1, rows):
         total_sq = total_sq + sq_in[k]
@@ -142,7 +151,7 @@
         w_copy(q, False).wait()
         core_out[q] = jnp.dot(x_ref[...], w_partner[q % PAIRS], preferred_element_type=jnp.float32)
 
-        @pl.when(q + PAIRS < 2 * tiles)
+        @pl.when(q + PAIRS < partner_count + tiles)
         def _():
             w_copy(q + PAIRS, False).start()
 
@@ -152,7 +161,7 @@
         w_copy(q, True).wait()
         total[...] = jnp.dot(x_ref[...], w_own[q % PAIRS], preferred_element_type=jnp.float32)
 
-        @pl.when(q + PAIRS < 2 * tiles)
+        @pl.when(q + PAIRS < own_count + tiles)
         def _():
             w_copy(q + PAIRS, True).start()
 
@@ -162,24 +171,34 @@
     def columns(i):
         return pl.ds(pl.multiple_of(i * TILE, TILE), TILE)
 
+    def send_tile(s):
+        own_tile(s, chip_out.at[s])
+        chip_copy(s).start()
+
+    def keep_tile(s):
+        own_tile(s, z_ref.at[:, columns(s - own_count)])
+
     partner_tile(0)
 
-    @pl.loop(0, tiles)
-    def _(q):
-        partner_tile(q + 1)
-        own_tile(q, chip_out.at[q])
-        chip_copy(q).start()
-
-    @pl.loop(0, tiles - 1)
-    def _(i):
-        partner_tile(tiles + i + 1)
-        own_tile(tiles + i, z_ref.at[:, columns(i)])
-
-    own_tile(2 * tiles - 1, z_ref.at[:, (tiles - 1) * TILE:])
+    @pl.loop(0, tiles - SHIFT)
+    def _(s):
+        partner_tile(s + 1)
+        send_tile(s)
+
+    @pl.loop(tiles - SHIFT, tiles + SHIFT)
+    def _(s):
+        partner_tile(s + 1)
+        pl.when(core == 1)(lambda: send_tile(s))
+        pl.when(core == 0)(lambda: keep_tile(s))
+
+    @pl.loop(tiles + SHIFT, 2 * tiles + SHIFT)
+    def _(s):
+        pl.when(s + 1 < partner_count + tiles)(lambda: partner_tile(s + 1))
+        pl.when(s < own_count + tiles)(lambda: keep_tile(s))
 
     def finish(i, carry):
         peak, mass = carry
-        chip_copy(i).wait_recv()
+        chip_arrival(i).wait_recv()
         z = z_ref[:, columns(i)] + chip_in[i]
         z_ref[:, columns(i)] = z
         parts = [z[:, k * LANES:(k + 1) * LANES] for k in range(TILE // LANES)]
@@ -199,17 +218,31 @@
     mass_out[...] = message
     mass_in[me] = message
 
-    for k in range(1, everyone):
-        pltpu.make_async_remote_copy(
-            mass_out, mass_in.at[me], mass_send.at[k], mass_recv.at[me],
-            device_id=peers[k - 1], device_id_type=MESH,
-        ).start()
-    for k in range(1, everyone):
-        other = (me + k) % everyone
-        pltpu.make_async_remote_copy(
-            mass_out, mass_in.at[other], mass_send.at[k], mass_recv.at[other],
-            device_id=peers[k - 1], device_id_type=MESH,
-        ).wait_recv()
+    def mass_copy(k, arrival=False):
+        peer, place = peers[k]
+        slot = place if arrival else me
+        return pltpu.make_async_remote_copy(
+            mass_out, mass_in.at[slot], mass_send.at[k], mass_recv.at[slot],
+            device_id=peer, device_id_type=MESH,
+        )
+
+    everyone = cols * rows
+    for k in range(everyone - 1):
+        mass_copy(k).start()
+
+    for k in range(rows - 1):
+        sq_copy(k).wait_send()
+
+    @pl.loop(0, partner_count + tiles)
+    def _(s):
+        core_copy(s).wait_send()
+
+    @pl.loop(0, own_count)
+    def _(s):
+        chip_copy(s).wait_send()
+
+    for k in reversed(range(everyone - 1)):
+        mass_copy(k, arrival=True).wait_recv()
     peaks = [mass_in[d, 0:1] for d in range(everyone)]
     top = functools.reduce(jnp.maximum, peaks)
     total = jnp.zeros_like(top)
@@ -219,32 +252,22 @@
     lse_row_ref[...] = log_norm
     lse_col_ref[...] = jnp.broadcast_to(log_norm, (LANES, LANES)).T[:batch]
 
-    for k in range(1, rows):
-        sq_copy(k).wait_send()
-    for k in range(1, everyone):
-        pltpu.make_async_remote_copy(
-            mass_out, mass_in.at[me], mass_send.at[k], mass_recv.at[me],
-            device_id=peers[k - 1], device_id_type=MESH,
-        ).wait_send()
-
-    @pl.loop(0, tiles)
-    def _(i):
-        core_copy(i).wait_send()
-        core_copy(tiles + i).wait_send()
-        chip_copy(i).wait_send()
-
-
-def subtract_kernel(z_ref, lse_col_ref, lse_row_ref, out_hbm, log_norm_ref, out_ref, sem):
+    for k in range(everyone - 1):
+        mass_copy(k).wait_send()
+
+
+def subtract_kernel(z_ref, lse_col_ref, lse_row_ref, out_hbm, log_norm_hbm, out_ref, log_norm_ref, sem, log_norm_sem):
     batch, block = z_ref.shape
     lse = lse_col_ref[...]
-    copies = []
+    log_norm_ref[...] = lse_row_ref[0, :batch]
+    copies = [pltpu.make_async_copy(log_norm_ref, log_norm_hbm, log_norm_sem)]
+    copies[0].start()
     for n in range(CHUNKS):
         for k in range(n * block // CHUNKS, (n + 1) * block // CHUNKS, LANES):
             out_ref[:, k:k + LANES] = z_ref[:, k:k + LANES] - lse
         at = pl.ds(n * block // CHUNKS, block // CHUNKS)
         copies.append(pltpu.make_async_copy(out_ref.at[:, at], out_hbm.at[:, at], sem.at[n]))
         copies[-1].start()
-    log_norm_ref[...] = lse_row_ref[0, :batch]
     for copy in copies:
         copy.wait()
 
@@ -277,9 +300,9 @@
                 pltpu.VMEM((batch, width), jnp.bfloat16),
                 pltpu.VMEM((PAIRS, width, TILE), jnp.bfloat16),
                 pltpu.VMEM((PAIRS, width, TILE), jnp.bfloat16),
-                pltpu.VMEM((2 * tiles, batch, TILE), f32),
-                pltpu.VMEM((2 * tiles, batch, TILE), f32),
-                pltpu.VMEM((tiles, batch, TILE), f32),
+                pltpu.VMEM((2 * tiles + SHIFT, batch, TILE), f32),
+                pltpu.VMEM((2 * tiles + SHIFT, batch, TILE), f32),
+                pltpu.VMEM((tiles + SHIFT, batch, TILE), f32),
                 pltpu.VMEM((tiles, batch, TILE), f32),
                 pltpu.VMEM((1, LANES), f32),
                 pltpu.VMEM((rows, 1, LANES), f32),
@@ -289,9 +312,9 @@
                 dma,
                 dma((PAIRS,)),
                 dma((PAIRS,)),
-                dma((2 * tiles,)),
-                dma((2 * tiles,)),
-                dma((tiles,)),
+                dma((2 * tiles + SHIFT,)),
+                dma((2 * tiles + SHIFT,)),
+                dma((tiles + SHIFT,)),
                 dma((tiles,)),
                 dma((rows,)),
                 dma((rows,)),
@@ -310,8 +333,8 @@
                 jax.ShapeDtypeStruct((batch,), f32),
             ),
             in_specs=[vmem] * 3,
-            out_specs=[hbm, vmem],
-            scratch_shapes=[pltpu.VMEM((batch, block), f32), dma((CHUNKS,))],
+            out_specs=[hbm] * 2,
+            scratch_shapes=[pltpu.VMEM((batch, block), f32), pltpu.VMEM((batch,), f32), dma((CHUNKS,)), dma],
             compiler_params=pltpu.CompilerParams(vmem_limit_bytes=16 * 1024 * 1024),
         )(z, lse_col, lse_row)
 

time: 109 us -> 108 us (level)
  no operation moved by 1% of the time
where the time goes in v4:
time: 108 us
  Pallas kernels  107 us (99%)
    pallas_call x1, Pallas kernels, local_head(): pl.pallas_call(functools.partial(head_kernel, sizes), name='head', out_sh...  105 us

profile of v4, /device:TPU:0, one launch (start us, length us, event | category | flops | bytes accessed | tf_op | source)
XLA Modules:
  0.0 107.7 jit_solution(13301219176872495220)
XLA Ops:
  0.6 105.0 %head.1 = (f32[64,16384]{1,0:T(8,128)S(1)}, f32[64,128]{1,0:T(8,128)S(1)}, f32[1,128]{1,0:T(1,128)S(1)}) custom-call(bf16[64,1280]{1,0:T(8,128)(2,1)} %hidden_hbm.1, f32[1280]{0:T(1024)} %gain_hbm.1, bf16[1280,65536]{1,0:T(8,128)(2,1)} %w_hbm.1), custom_call_target="tpu_custom_call" | custom-call | tf_op jit(solution)/shard_map/head/pallas_call | solution.py:287
  105.6 2.1 %subtract.1 = (f32[64,16384]{1,0:T(8,128)}, f32[64]{0:T(128)}) custom-call(f32[64,16384]{1,0:T(8,128)S(1)} %get-tuple-element.5.z_ref, f32[64,128]{1,0:T(8,128)S(1)} %get-tuple-element.6.lse_col_ref, f32[1,128]{1,0:T(1,128)S(1)} %get-tuple-element.7.lse_row_ref), custom_call_target="tpu_custom_call" | custom-call | tf_op jit(solution)/shard_map/subtract/pallas_call | solution.py:328

commit v5 on v4

--- a/solution.py
+++ b/solution.py
@@ -12,9 +12,23 @@
 LANES = 128
 TILE = 512
 PAIRS = 6
-SHIFT = 1
+SHIFT = 0
 CHUNKS = 8
 VMEM_LIMIT = 48 * 1024 * 1024
+
+
+def diagonal(batch):
+    shape = (batch, batch)
+    return lax.broadcasted_iota(jnp.int32, shape, 0) == lax.broadcasted_iota(jnp.int32, shape, 1)
+
+
+def column_to_row(column):
+    batch = column.shape[0]
+    return jnp.sum(jnp.where(diagonal(batch), column, 0.0), axis=0, keepdims=True)
+
+
+def row_to_column(row):
+    return jnp.sum(jnp.where(diagonal(row.shape[1]), row, 0.0), axis=1, keepdims=True)
 
 
 def head_kernel(
@@ -121,7 +135,7 @@
     for k in range(width // LANES):
         part = h_ref[:, k * LANES:(k + 1) * LANES].astype(jnp.float32)
         squares = squares + part * part
-    local_sq = jnp.sum(jnp.concatenate([squares, squares], axis=0).T, axis=0, keepdims=True)
+    local_sq = column_to_row(jnp.sum(squares, axis=1, keepdims=True))
     sq_out[...] = local_sq
     sq_in[row] = local_sq
     pl.semaphore_wait(barrier, rows)
@@ -142,7 +156,7 @@
     for k in range(1, rows):
         total_sq = total_sq + sq_in[k]
     scale_row = lax.rsqrt(total_sq / features + EPS)
-    scale = jnp.broadcast_to(scale_row, (LANES, LANES)).T[:batch]
+    scale = row_to_column(scale_row)
     for k in range(width // LANES):
         at = slice(k * LANES, (k + 1) * LANES)
         x_ref[:, at] = (h_ref[:, at].astype(jnp.float32) * scale * gain_ref[at]).astype(jnp.bfloat16)
@@ -210,11 +224,11 @@
 
     start = (jnp.full((batch, LANES), -jnp.inf, jnp.float32), jnp.zeros((batch, LANES), jnp.float32))
     lane_peak, lane_mass = lax.fori_loop(0, tiles, finish, start)
-    peak = jnp.max(lane_peak, axis=1, keepdims=True)
-    mass = jnp.sum(lane_mass * jnp.exp(lane_peak - peak), axis=1, keepdims=True)
-    lane = lax.broadcasted_iota(jnp.int32, (batch, LANES), 1)
-    pair = jnp.where(lane == 0, peak, mass)
-    message = jnp.concatenate([pair, pair], axis=0).T[:8]
+    peaks_by_lane, mass_by_lane = lane_peak.T, lane_mass.T
+    peak = jnp.max(peaks_by_lane, axis=0, keepdims=True)
+    mass = jnp.sum(mass_by_lane * jnp.exp(peaks_by_lane - peak), axis=0, keepdims=True)
+    first = lax.broadcasted_iota(jnp.int32, (8, batch), 0) == 0
+    message = jnp.where(first, peak, mass)
     mass_out[...] = message
     mass_in[me] = message
 
@@ -250,7 +264,7 @@
         total = total + mass_in[d, 1:2] * jnp.exp(peaks[d] - top)
     log_norm = top + jnp.log(total)
     lse_row_ref[...] = log_norm
-    lse_col_ref[...] = jnp.broadcast_to(log_norm, (LANES, LANES)).T[:batch]
+    lse_col_ref[...] = jnp.broadcast_to(row_to_column(log_norm), (batch, LANES))
 
     for k in range(everyone - 1):
         mass_copy(k).wait_send()
@@ -259,7 +273,7 @@
 def subtract_kernel(z_ref, lse_col_ref, lse_row_ref, out_hbm, log_norm_hbm, out_ref, log_norm_ref, sem, log_norm_sem):
     batch, block = z_ref.shape
     lse = lse_col_ref[...]
-    log_norm_ref[...] = lse_row_ref[0, :batch]
+    log_norm_ref[...] = lse_row_ref[0]
     copies = [pltpu.make_async_copy(log_norm_ref, log_norm_hbm, log_norm_sem)]
     copies[0].start()
     for n in range(CHUNKS):
@@ -290,7 +304,7 @@
             out_shape=(
                 pltpu.VMEM((batch, block), f32),
                 pltpu.VMEM((batch, LANES), f32),
-                pltpu.VMEM((1, LANES), f32),
+                pltpu.VMEM((1, batch), f32),
             ),
             in_specs=[pl.BlockSpec(memory_space=pltpu.HBM)] * 3,
             out_specs=[vmem] * 3,
@@ -304,10 +318,10 @@
                 pltpu.VMEM((2 * tiles + SHIFT, batch, TILE), f32),
                 pltpu.VMEM((tiles + SHIFT, batch, TILE), f32),
                 pltpu.VMEM((tiles, batch, TILE), f32),
-                pltpu.VMEM((1, LANES), f32),
-                pltpu.VMEM((rows, 1, LANES), f32),
-                pltpu.VMEM((8, LANES), f32),
-                pltpu.VMEM((cols * rows, 8, LANES), f32),
+                pltpu.VMEM((1, batch), f32),
+                pltpu.VMEM((rows, 1, batch), f32),
+                pltpu.VMEM((8, batch), f32),
+                pltpu.VMEM((cols * rows, 8, batch), f32),
                 dma,
                 dma,
                 dma((PAIRS,)),

time: 108 us -> 108 us (level)
  no operation moved by 1% of the time
where the time goes in v5:
time: 108 us
  Pallas kernels  108 us (100%)
    pallas_call x1, Pallas kernels, local_head(): pl.pallas_call(functools.partial(head_kernel, sizes), name='head', out_sh...  105 us

profile of v5, /device:TPU:0, one launch (start us, length us, event | category | flops | bytes accessed | tf_op | source)
XLA Modules:
  0.0 108.2 jit_solution(8592168236264401803)
XLA Ops:
  0.6 105.5 %head.1 = (f32[64,16384]{1,0:T(8,128)S(1)}, f32[64,128]{1,0:T(8,128)S(1)}, f32[1,64]{1,0:T(1,128)S(1)}) custom-call(bf16[64,1280]{1,0:T(8,128)(2,1)} %hidden_hbm.1, f32[1280]{0:T(1024)} %gain_hbm.1, bf16[1280,65536]{1,0:T(8,128)(2,1)} %w_hbm.1), custom_call_target="tpu_custom_call" | custom-call | tf_op jit(solution)/shard_map/head/pallas_call | solution.py:301
  106.1 2.1 %subtract.1 = (f32[64,16384]{1,0:T(8,128)}, f32[64]{0:T(128)}) custom-call(f32[64,16384]{1,0:T(8,128)S(1)} %get-tuple-element.5.z_ref, f32[64,128]{1,0:T(8,128)S(1)} %get-tuple-element.6.lse_col_ref, f32[1,64]{1,0:T(1,128)S(1)} %get-tuple-element.7.lse_row_ref), custom_call_target="tpu_custom_call" | custom-call | tf_op jit(solution)/shard_map/subtract/pallas_call | solution.py:342

commit v6 on v5

--- a/solution.py
+++ b/solution.py
@@ -10,9 +10,9 @@
 EPS = 1e-5
 MESH = pl.DeviceIdType.MESH
 LANES = 128
-TILE = 512
-PAIRS = 6
-SHIFT = 0
+TILE = 256
+PAIRS = 12
+SHIFT = 1
 CHUNKS = 8
 VMEM_LIMIT = 48 * 1024 * 1024
 

time: 108 us -> 109 us (level)
  no operation moved by 1% of the time
where the time goes in v6:
time: 109 us
  Pallas kernels  108 us (99%)
    pallas_call x1, Pallas kernels, local_head(): pl.pallas_call(functools.partial(head_kernel, sizes), name='head', out_sh...  106 us

profile of v6, /device:TPU:0, one launch (start us, length us, event | category | flops | bytes accessed | tf_op | source)
XLA Modules:
  0.0 109.0 jit_solution(14596304025217596629)
XLA Ops:
  0.6 106.2 %head.1 = (f32[64,16384]{1,0:T(8,128)S(1)}, f32[64,128]{1,0:T(8,128)S(1)}, f32[1,64]{1,0:T(1,128)S(1)}) custom-call(bf16[64,1280]{1,0:T(8,128)(2,1)} %hidden_hbm.1, f32[1280]{0:T(1024)} %gain_hbm.1, bf16[1280,65536]{1,0:T(8,128)(2,1)} %w_hbm.1), custom_call_target="tpu_custom_call" | custom-call | tf_op jit(solution)/shard_map/head/pallas_call | solution.py:301
  106.8 2.1 %subtract.1 = (f32[64,16384]{1,0:T(8,128)}, f32[64]{0:T(128)}) custom-call(f32[64,16384]{1,0:T(8,128)S(1)} %get-tuple-element.5.z_ref, f32[64,128]{1,0:T(8,128)S(1)} %get-tuple-element.6.lse_col_ref, f32[1,64]{1,0:T(1,128)S(1)} %get-tuple-element.7.lse_row_ref), custom_call_target="tpu_custom_call" | custom-call | tf_op jit(solution)/shard_map/subtract/pallas_call | solution.py:342

commit v7 on v5

--- a/solution.py
+++ b/solution.py
@@ -12,7 +12,8 @@
 LANES = 128
 TILE = 512
 PAIRS = 6
-SHIFT = 0
+GROUP = 4
+SHIFT = 1
 CHUNKS = 8
 VMEM_LIMIT = 48 * 1024 * 1024
 
@@ -52,6 +53,8 @@
     sq_in,
     mass_out,
     mass_in,
+    lane_peak,
+    lane_mass,
     h_sem,
     gain_sem,
     w_own_sem,
@@ -102,18 +105,27 @@
             device_id=partner, device_id_type=MESH,
         )
 
-    def chip_copy(s):
+    def chip_copy(group, s, count):
         tile = core * (tiles - SHIFT) + s
+        place = core * tail if isinstance(group, int) and group == 0 else group
         return pltpu.make_async_remote_copy(
-            chip_out.at[s], chip_in.at[tile % tiles], chip_send.at[s], chip_recv.at[tile % tiles],
+            chip_out.at[pl.ds(s, count)], chip_in.at[pl.ds(tile % tiles, count)],
+            chip_send.at[group], chip_recv.at[place],
             device_id=(dp, col, (1 - chip) * 2 + tile // tiles), device_id_type=MESH,
         )
 
-    def chip_arrival(i):
+    def chip_arrival(place, first, count):
         return pltpu.make_async_remote_copy(
-            chip_out.at[0], chip_in.at[i], chip_send.at[0], chip_recv.at[i],
+            chip_out.at[pl.ds(0, count)], chip_in.at[pl.ds(first, count)],
+            chip_send.at[0], chip_recv.at[place],
             device_id=row_peers[1][0], device_id_type=MESH,
         )
+
+    def group_start(group):
+        return (group - 2) * GROUP + 3
+
+    last_group = 2 + (tiles - SHIFT - 3) // GROUP
+    tail = last_group + 1
 
     h_copy = pltpu.make_async_copy(hidden_hbm, h_ref, h_sem)
     gain_copy = pltpu.make_async_copy(gain_hbm, gain_ref, gain_sem)
@@ -187,17 +199,29 @@
 
     def send_tile(s):
         own_tile(s, chip_out.at[s])
-        chip_copy(s).start()
 
     def keep_tile(s):
         own_tile(s, z_ref.at[:, columns(s - own_count)])
 
     partner_tile(0)
 
-    @pl.loop(0, tiles - SHIFT)
+    @pl.loop(0, 3)
     def _(s):
         partner_tile(s + 1)
         send_tile(s)
+        pl.when(s == 0)(lambda: chip_copy(0, 0, 1).start())
+
+    chip_copy(1, 1, 2).start()
+
+    @pl.loop(2, last_group)
+    def _(group):
+        @pl.loop(0, GROUP)
+        def _(t):
+            s = group_start(group) + t
+            partner_tile(s + 1)
+            send_tile(s)
+
+        chip_copy(group, group_start(group), GROUP).start()
 
     @pl.loop(tiles - SHIFT, tiles + SHIFT)
     def _(s):
@@ -205,26 +229,46 @@
         pl.when(core == 1)(lambda: send_tile(s))
         pl.when(core == 0)(lambda: keep_tile(s))
 
+    pl.when(core == 1)(lambda: chip_copy(last_group, tiles - SHIFT, 2 * SHIFT).start())
+
     @pl.loop(tiles + SHIFT, 2 * tiles + SHIFT)
     def _(s):
         pl.when(s + 1 < partner_count + tiles)(lambda: partner_tile(s + 1))
         pl.when(s < own_count + tiles)(lambda: keep_tile(s))
 
-    def finish(i, carry):
-        peak, mass = carry
-        chip_arrival(i).wait_recv()
-        z = z_ref[:, columns(i)] + chip_in[i]
-        z_ref[:, columns(i)] = z
-        parts = [z[:, k * LANES:(k + 1) * LANES] for k in range(TILE // LANES)]
-        new_peak = functools.reduce(jnp.maximum, parts, peak)
-        mass = mass * jnp.exp(peak - new_peak)
-        for part in parts:
-            mass = mass + jnp.exp(part - new_peak)
-        return new_peak, mass
-
-    start = (jnp.full((batch, LANES), -jnp.inf, jnp.float32), jnp.zeros((batch, LANES), jnp.float32))
-    lane_peak, lane_mass = lax.fori_loop(0, tiles, finish, start)
-    peaks_by_lane, mass_by_lane = lane_peak.T, lane_mass.T
+    lane_peak[...] = jnp.full((batch, LANES), -jnp.inf, jnp.float32)
+    lane_mass[...] = jnp.zeros((batch, LANES), jnp.float32)
+
+    def finish(place, first, count):
+        chip_arrival(place, first, count).wait_recv()
+
+        @pl.loop(first, first + count)
+        def _(i):
+            z = z_ref[:, columns(i)] + chip_in[i]
+            z_ref[:, columns(i)] = z
+            parts = [z[:, k * LANES:(k + 1) * LANES] for k in range(TILE // LANES)]
+            peak = lane_peak[...]
+            new_peak = functools.reduce(jnp.maximum, parts, peak)
+            mass = lane_mass[...] * jnp.exp(peak - new_peak)
+            for part in parts:
+                mass = mass + jnp.exp(part - new_peak)
+            lane_peak[...] = new_peak
+            lane_mass[...] = mass
+
+    @pl.when(core == 0)
+    def _():
+        finish(0, 0, 1)
+        finish(tail, tiles - 1, 1)
+
+    finish(1, 1 - core, 2)
+
+    @pl.loop(2, last_group)
+    def _(group):
+        finish(group, group_start(group) - core, GROUP)
+
+    pl.when(core == 1)(lambda: finish(last_group, tiles - 2 * SHIFT, 2 * SHIFT))
+
+    peaks_by_lane, mass_by_lane = lane_peak[...].T, lane_mass[...].T
     peak = jnp.max(peaks_by_lane, axis=0, keepdims=True)
     mass = jnp.sum(mass_by_lane * jnp.exp(peaks_by_lane - peak), axis=0, keepdims=True)
     first = lax.broadcasted_iota(jnp.int32, (8, batch), 0) == 0
@@ -251,9 +295,14 @@
     def _(s):
         core_copy(s).wait_send()
 
-    @pl.loop(0, own_count)
-    def _(s):
-        chip_copy(s).wait_send()
+    chip_copy(0, 0, 1).wait_send()
+    chip_copy(1, 1, 2).wait_send()
+
+    @pl.loop(2, last_group)
+    def _(group):
+        chip_copy(group, group_start(group), GROUP).wait_send()
+
+    pl.when(core == 1)(lambda: chip_copy(last_group, tiles - SHIFT, 2 * SHIFT).wait_send())
 
     for k in reversed(range(everyone - 1)):
         mass_copy(k, arrival=True).wait_recv()
@@ -322,6 +371,8 @@
                 pltpu.VMEM((rows, 1, batch), f32),
                 pltpu.VMEM((8, batch), f32),
                 pltpu.VMEM((cols * rows, 8, batch), f32),
+                pltpu.VMEM((batch, LANES), f32),
+                pltpu.VMEM((batch, LANES), f32),
                 dma,
                 dma,
                 dma((PAIRS,)),

time: 108 us -> 108 us (level)
  no operation moved by 1% of the time
where the time goes in v7:
time: 108 us
  Pallas kernels  107 us (99%)
    pallas_call x1, Pallas kernels, local_head(): pl.pallas_call(functools.partial(head_kernel, sizes), name='head', out_sh...  105 us

profile of v7, /device:TPU:0, one launch (start us, length us, event | category | flops | bytes accessed | tf_op | source)
XLA Modules:
  0.0 107.7 jit_solution(1740020202925164569)
XLA Ops:
  0.6 105.0 %head.1 = (f32[64,16384]{1,0:T(8,128)S(1)}, f32[64,128]{1,0:T(8,128)S(1)}, f32[1,64]{1,0:T(1,128)S(1)}) custom-call(bf16[64,1280]{1,0:T(8,128)(2,1)} %hidden_hbm.1, f32[1280]{0:T(1024)} %gain_hbm.1, bf16[1280,65536]{1,0:T(8,128)(2,1)} %w_hbm.1), custom_call_target="tpu_custom_call" | custom-call | tf_op jit(solution)/shard_map/head/pallas_call | solution.py:350
  105.6 2.1 %subtract.1 = (f32[64,16384]{1,0:T(8,128)}, f32[64]{0:T(128)}) custom-call(f32[64,16384]{1,0:T(8,128)S(1)} %get-tuple-element.5.z_ref, f32[64,128]{1,0:T(8,128)S(1)} %get-tuple-element.6.lse_col_ref, f32[1,64]{1,0:T(1,128)S(1)} %get-tuple-element.7.lse_row_ref), custom_call_target="tpu_custom_call" | custom-call | tf_op jit(solution)/shard_map/subtract/pallas_call | solution.py:393

commit v8 on v7

--- a/solution.py
+++ b/solution.py
@@ -13,8 +13,9 @@
 TILE = 512
 PAIRS = 6
 GROUP = 4
+EARLY = 2
 SHIFT = 1
-CHUNKS = 8
+CHUNKS = 16
 VMEM_LIMIT = 48 * 1024 * 1024
 
 
@@ -136,10 +137,13 @@
     for peer, _ in [mirror, *row_peers]:
         pl.semaphore_signal(barrier, inc=1, device_id=peer, device_id_type=MESH)
 
-    @pl.loop(0, PAIRS)
-    def _(q):
-        w_copy(q, False).start()
-        w_copy(q, True).start()
+    def fetch(first, last):
+        @pl.loop(first, last)
+        def _(q):
+            w_copy(q, False).start()
+            w_copy(q, True).start()
+
+    fetch(0, EARLY)
 
     h_copy.wait()
     gain_copy.wait()
@@ -162,6 +166,7 @@
 
     for k in range(rows - 1):
         sq_copy(k).start()
+    fetch(EARLY, PAIRS)
     for k in reversed(range(rows - 1)):
         sq_copy(k, arrival=True).wait_recv()
     total_sq = sq_in[0]
@@ -271,7 +276,7 @@
     peaks_by_lane, mass_by_lane = lane_peak[...].T, lane_mass[...].T
     peak = jnp.max(peaks_by_lane, axis=0, keepdims=True)
     mass = jnp.sum(mass_by_lane * jnp.exp(peaks_by_lane - peak), axis=0, keepdims=True)
-    first = lax.broadcasted_iota(jnp.int32, (8, batch), 0) == 0
+    first = lax.broadcasted_iota(jnp.int32, (2, batch), 0) == 0
     message = jnp.where(first, peak, mass)
     mass_out[...] = message
     mass_in[me] = message
@@ -369,8 +374,8 @@
                 pltpu.VMEM((tiles, batch, TILE), f32),
                 pltpu.VMEM((1, batch), f32),
                 pltpu.VMEM((rows, 1, batch), f32),
-                pltpu.VMEM((8, batch), f32),
-                pltpu.VMEM((cols * rows, 8, batch), f32),
+                pltpu.VMEM((2, batch), f32),
+                pltpu.VMEM((cols * rows, 2, batch), f32),
                 pltpu.VMEM((batch, LANES), f32),
                 pltpu.VMEM((batch, LANES), f32),
                 dma,

time: 108 us -> 108 us (level)
  no operation moved by 1% of the time
where the time goes in v8:
time: 108 us
  Pallas kernels  107 us (99%)
    pallas_call x1, Pallas kernels, local_head(): pl.pallas_call(functools.partial(head_kernel, sizes), name='head', out_sh...  105 us
    pallas_call x1, Pallas kernels, local_head(): pl.pallas_call(subtract_kernel, name='subtract', out_shape=(jax.ShapeDtyp...  2.17 us

profile of v8, /device:TPU:0, one launch (start us, length us, event | category | flops | bytes accessed | tf_op | source)
XLA Modules:
  0.0 107.7 jit_solution(15781569421651012859)
XLA Ops:
  0.6 104.9 %head.1 = (f32[64,16384]{1,0:T(8,128)S(1)}, f32[64,128]{1,0:T(8,128)S(1)}, f32[1,64]{1,0:T(1,128)S(1)}) custom-call(bf16[64,1280]{1,0:T(8,128)(2,1)} %hidden_hbm.1, f32[1280]{0:T(1024)} %gain_hbm.1, bf16[1280,65536]{1,0:T(8,128)(2,1)} %w_hbm.1), custom_call_target="tpu_custom_call" | custom-call | tf_op jit(solution)/shard_map/head/pallas_call | solution.py:355
  105.6 2.2 %subtract.1 = (f32[64,16384]{1,0:T(8,128)}, f32[64]{0:T(128)}) custom-call(f32[64,16384]{1,0:T(8,128)S(1)} %get-tuple-element.5.z_ref, f32[64,128]{1,0:T(8,128)S(1)} %get-tuple-element.6.lse_col_ref, f32[1,64]{1,0:T(1,128)S(1)} %get-tuple-element.7.lse_row_ref), custom_call_target="tpu_custom_call" | custom-call | tf_op jit(solution)/shard_map/subtract/pallas_call | solution.py:398

commit v9 on v8

--- a/solution.py
+++ b/solution.py
@@ -14,8 +14,9 @@
 PAIRS = 6
 GROUP = 4
 EARLY = 2
+EDGE = 128
 SHIFT = 1
-CHUNKS = 16
+SUBLANES = 8
 VMEM_LIMIT = 48 * 1024 * 1024
 
 
@@ -56,6 +57,12 @@
     mass_in,
     lane_peak,
     lane_mass,
+    w_edge,
+    edge_out,
+    edge_in,
+    edge_sem,
+    edge_send,
+    edge_recv,
     h_sem,
     gain_sem,
     w_own_sem,
@@ -100,26 +107,46 @@
             w_hbm.at[:, pl.ds(pl.multiple_of(start, TILE), TILE)], buf.at[slot], sem.at[slot]
         )
 
-    def core_copy(s):
-        return pltpu.make_async_remote_copy(
-            core_out.at[s], core_in.at[s], core_send.at[s], core_recv.at[s],
+    def core_copy(s, cut=0):
+        at = pl.ds(cut, TILE - cut)
+        return pltpu.make_async_remote_copy(
+            core_out.at[s, :, at], core_in.at[s, :, at], core_send.at[s], core_recv.at[s],
             device_id=partner, device_id_type=MESH,
         )
 
-    def chip_copy(group, s, count):
+    def chip_copy(group, s, count, cut=0):
+        at = pl.ds(cut, TILE - cut)
         tile = core * (tiles - SHIFT) + s
         place = core * tail if isinstance(group, int) and group == 0 else group
         return pltpu.make_async_remote_copy(
-            chip_out.at[pl.ds(s, count)], chip_in.at[pl.ds(tile % tiles, count)],
+            chip_out.at[pl.ds(s, count), :, at], chip_in.at[pl.ds(tile % tiles, count), :, at],
             chip_send.at[group], chip_recv.at[place],
             device_id=(dp, col, (1 - chip) * 2 + tile // tiles), device_id_type=MESH,
         )
 
-    def chip_arrival(place, first, count):
-        return pltpu.make_async_remote_copy(
-            chip_out.at[pl.ds(0, count)], chip_in.at[pl.ds(first, count)],
+    def chip_arrival(place, first, count, cut=0):
+        at = pl.ds(cut, TILE - cut)
+        return pltpu.make_async_remote_copy(
+            chip_out.at[pl.ds(0, count), :, at], chip_in.at[pl.ds(first, count), :, at],
             chip_send.at[0], chip_recv.at[place],
             device_id=row_peers[1][0], device_id_type=MESH,
+        )
+
+    def edge_start(own):
+        side = core if own else 1 - core
+        start = (1 - chip) * 2 * block + side * (tiles - SHIFT) * TILE
+        return pl.ds(pl.multiple_of(start, TILE), EDGE)
+
+    def edge_fetch(k):
+        return pltpu.make_async_copy(
+            w_hbm.at[:, edge_start(k == 0)], w_edge.at[:, pl.ds(k * EDGE, EDGE)], edge_sem.at[k]
+        )
+
+    def edge_copy(k, arrival=None):
+        place = arrival if arrival is not None else 2 * core if k == 0 else 3 - 2 * core
+        return pltpu.make_async_remote_copy(
+            edge_out.at[k], edge_in.at[place], edge_send.at[k], edge_recv.at[place],
+            device_id=(dp, col, (1 - chip) * 2), device_id_type=MESH,
         )
 
     def group_start(group):
@@ -143,6 +170,8 @@
             w_copy(q, False).start()
             w_copy(q, True).start()
 
+    edge_fetch(0).start()
+    edge_fetch(1).start()
     fetch(0, EARLY)
 
     h_copy.wait()
@@ -178,26 +207,26 @@
         at = slice(k * LANES, (k + 1) * LANES)
         x_ref[:, at] = (h_ref[:, at].astype(jnp.float32) * scale * gain_ref[at]).astype(jnp.bfloat16)
 
-    def partner_tile(q):
+    def partner_tile(q, cut=0):
         w_copy(q, False).wait()
-        core_out[q] = jnp.dot(x_ref[...], w_partner[q % PAIRS], preferred_element_type=jnp.float32)
+        core_out[q, :, cut:] = jnp.dot(x_ref[...], w_partner[q % PAIRS, :, cut:], preferred_element_type=jnp.float32)
 
         @pl.when(q + PAIRS < partner_count + tiles)
         def _():
             w_copy(q + PAIRS, False).start()
 
-        core_copy(q).start()
-
-    def own_tile(q, total):
+        core_copy(q, cut).start()
+
+    def own_tile(q, total, cut=0):
         w_copy(q, True).wait()
-        total[...] = jnp.dot(x_ref[...], w_own[q % PAIRS], preferred_element_type=jnp.float32)
+        total[...] = jnp.dot(x_ref[...], w_own[q % PAIRS, :, cut:], preferred_element_type=jnp.float32)
 
         @pl.when(q + PAIRS < own_count + tiles)
         def _():
             w_copy(q + PAIRS, True).start()
 
-        core_copy(q).wait_recv()
-        total[...] += core_in[q]
+        core_copy(q, cut).wait_recv()
+        total[...] += core_in[q, :, cut:]
 
     def columns(i):
         return pl.ds(pl.multiple_of(i * TILE, TILE), TILE)
@@ -208,13 +237,21 @@
     def keep_tile(s):
         own_tile(s, z_ref.at[:, columns(s - own_count)])
 
-    partner_tile(0)
-
-    @pl.loop(0, 3)
+    edge_fetch(0).wait()
+    edge_fetch(1).wait()
+    edge = jnp.dot(x_ref[...], w_edge[...], preferred_element_type=jnp.float32)
+    for k in range(2):
+        edge_out[k] = edge[:, k * EDGE:(k + 1) * EDGE]
+        edge_copy(k).start()
+    partner_tile(0, EDGE)
+    partner_tile(1)
+    own_tile(0, chip_out.at[0, :, pl.ds(EDGE, TILE - EDGE)], EDGE)
+    chip_copy(0, 0, 1, EDGE).start()
+
+    @pl.loop(1, 3)
     def _(s):
         partner_tile(s + 1)
         send_tile(s)
-        pl.when(s == 0)(lambda: chip_copy(0, 0, 1).start())
 
     chip_copy(1, 1, 2).start()
 
@@ -244,8 +281,14 @@
     lane_peak[...] = jnp.full((batch, LANES), -jnp.inf, jnp.float32)
     lane_mass[...] = jnp.zeros((batch, LANES), jnp.float32)
 
-    def finish(place, first, count):
-        chip_arrival(place, first, count).wait_recv()
+    def finish(place, first, count, edges=None):
+        if edges is None:
+            chip_arrival(place, first, count).wait_recv()
+        else:
+            for k in range(2):
+                edge_copy(k, arrival=edges + k).wait_recv()
+            chip_in[first, :, :EDGE] = edge_in[edges] + edge_in[edges + 1]
+            chip_arrival(place, first, count, EDGE).wait_recv()
 
         @pl.loop(first, first + count)
         def _(i):
@@ -262,8 +305,8 @@
 
     @pl.when(core == 0)
     def _():
-        finish(0, 0, 1)
-        finish(tail, tiles - 1, 1)
+        finish(0, 0, 1, edges=0)
+        finish(tail, tiles - 1, 1, edges=2)
 
     finish(1, 1 - core, 2)
 
@@ -296,11 +339,15 @@
     for k in range(rows - 1):
         sq_copy(k).wait_send()
 
-    @pl.loop(0, partner_count + tiles)
+    core_copy(0, EDGE).wait_send()
+
+    @pl.loop(1, partner_count + tiles)
     def _(s):
         core_copy(s).wait_send()
 
-    chip_copy(0, 0, 1).wait_send()
+    for k in range(2):
+        edge_copy(k).wait_send()
+    chip_copy(0, 0, 1, EDGE).wait_send()
     chip_copy(1, 1, 2).wait_send()
 
     @pl.loop(2, last_group)
@@ -326,15 +373,16 @@
 
 def subtract_kernel(z_ref, lse_col_ref, lse_row_ref, out_hbm, log_norm_hbm, out_ref, log_norm_ref, sem, log_norm_sem):
     batch, block = z_ref.shape
-    lse = lse_col_ref[...]
     log_norm_ref[...] = lse_row_ref[0]
     copies = [pltpu.make_async_copy(log_norm_ref, log_norm_hbm, log_norm_sem)]
     copies[0].start()
-    for n in range(CHUNKS):
-        for k in range(n * block // CHUNKS, (n + 1) * block // CHUNKS, LANES):
-            out_ref[:, k:k + LANES] = z_ref[:, k:k + LANES] - lse
-        at = pl.ds(n * block // CHUNKS, block // CHUNKS)
-        copies.append(pltpu.make_async_copy(out_ref.at[:, at], out_hbm.at[:, at], sem.at[n]))
+    for n in range(batch // SUBLANES):
+        at = slice(n * SUBLANES, (n + 1) * SUBLANES)
+        lse = lse_col_ref[at]
+        for k in range(0, block, LANES):
+            out_ref[at, k:k + LANES] = z_ref[at, k:k + LANES] - lse
+        rows = pl.ds(n * SUBLANES, SUBLANES)
+        copies.append(pltpu.make_async_copy(out_ref.at[rows], out_hbm.at[rows], sem.at[n]))
         copies[-1].start()
     for copy in copies:
         copy.wait()
@@ -378,6 +426,12 @@
                 pltpu.VMEM((cols * rows, 2, batch), f32),
                 pltpu.VMEM((batch, LANES), f32),
                 pltpu.VMEM((batch, LANES), f32),
+                pltpu.VMEM((width, 2 * EDGE), jnp.bfloat16),
+                pltpu.VMEM((2, batch, EDGE), f32),
+                pltpu.VMEM((4, batch, EDGE), f32),
+                dma((2,)),
+                dma((2,)),
+                dma((4,)),
                 dma,
                 dma,
                 dma((PAIRS,)),
@@ -404,7 +458,7 @@
             ),
             in_specs=[vmem] * 3,
             out_specs=[hbm] * 2,
-            scratch_shapes=[pltpu.VMEM((batch, block), f32), pltpu.VMEM((batch,), f32), dma((CHUNKS,)), dma],
+            scratch_shapes=[pltpu.VMEM((batch, block), f32), pltpu.VMEM((batch,), f32), dma((batch // SUBLANES,)), dma],
             compiler_params=pltpu.CompilerParams(vmem_limit_bytes=16 * 1024 * 1024),
         )(z, lse_col, lse_row)
 

time: 108 us -> 107 us (level)
  no operation moved by 1% of the time
where the time goes in v9:
time: 107 us
  Pallas kernels  107 us (100%)
    pallas_call x1, Pallas kernels, local_head(): pl.pallas_call(functools.partial(head_kernel, sizes), name='head', out_sh...  105 us

profile of v9, /device:TPU:0, one launch (start us, length us, event | category | flops | bytes accessed | tf_op | source)
XLA Modules:
  0.0 107.3 jit_solution(4299476676918627098)
XLA Ops:
  0.6 104.5 %head.1 = (f32[64,16384]{1,0:T(8,128)S(1)}, f32[64,128]{1,0:T(8,128)S(1)}, f32[1,64]{1,0:T(1,128)S(1)}) custom-call(bf16[64,1280]{1,0:T(8,128)(2,1)} %hidden_hbm.1, f32[1280]{0:T(1024)} %gain_hbm.1, bf16[1280,65536]{1,0:T(8,128)(2,1)} %w_hbm.1), custom_call_target="tpu_custom_call" | custom-call | tf_op jit(solution)/shard_map/head/pallas_call | solution.py:403
  105.2 2.1 %subtract.1 = (f32[64,16384]{1,0:T(8,128)}, f32[64]{0:T(128)}) custom-call(f32[64,16384]{1,0:T(8,128)S(1)} %get-tuple-element.5.z_ref, f32[64,128]{1,0:T(8,128)S(1)} %get-tuple-element.6.lse_col_ref, f32[1,64]{1,0:T(1,128)S(1)} %get-tuple-element.7.lse_row_ref), custom_call_target="tpu_custom_call" | custom-call | tf_op jit(solution)/shard_map/subtract/pallas_call | solution.py:452

commit v10 on v9

--- a/solution.py
+++ b/solution.py
@@ -239,7 +239,9 @@
 
     edge_fetch(0).wait()
     edge_fetch(1).wait()
-    edge = jnp.dot(x_ref[...], w_edge[...], preferred_element_type=jnp.float32)
+    half = width // 2
+    edge = jnp.dot(x_ref[:, :half], w_edge[:half], preferred_element_type=jnp.float32)
+    edge += jnp.dot(x_ref[:, half:], w_edge[half:], preferred_element_type=jnp.float32)
     for k in range(2):
         edge_out[k] = edge[:, k * EDGE:(k + 1) * EDGE]
         edge_copy(k).start()
@@ -255,8 +257,14 @@
 
     chip_copy(1, 1, 2).start()
 
+    def pace(group):
+        chip_arrival(group, group_start(group) - core, GROUP).wait_recv()
+
     @pl.loop(2, last_group)
     def _(group):
+        pl.when(group == 4)(lambda: chip_arrival(1, 1 - core, 2).wait_recv())
+        pl.when((group > 4) & (group % 2 == 0))(lambda: pace(group // 2 - 1))
+
         @pl.loop(0, GROUP)
         def _(t):
             s = group_start(group) + t
@@ -275,16 +283,18 @@
 
     @pl.loop(tiles + SHIFT, 2 * tiles + SHIFT)
     def _(s):
+        step = s - tiles - SHIFT
+        pl.when(step % (2 * GROUP) == GROUP)(lambda: pace(last_group // 2 + step // (2 * GROUP)))
         pl.when(s + 1 < partner_count + tiles)(lambda: partner_tile(s + 1))
         pl.when(s < own_count + tiles)(lambda: keep_tile(s))
 
     lane_peak[...] = jnp.full((batch, LANES), -jnp.inf, jnp.float32)
     lane_mass[...] = jnp.zeros((batch, LANES), jnp.float32)
 
-    def finish(place, first, count, edges=None):
-        if edges is None:
+    def finish(place, first, count, edges=None, wait=True):
+        if wait and edges is None:
             chip_arrival(place, first, count).wait_recv()
-        else:
+        if edges is not None:
             for k in range(2):
                 edge_copy(k, arrival=edges + k).wait_recv()
             chip_in[first, :, :EDGE] = edge_in[edges] + edge_in[edges + 1]
@@ -308,11 +318,13 @@
         finish(0, 0, 1, edges=0)
         finish(tail, tiles - 1, 1, edges=2)
 
-    finish(1, 1 - core, 2)
-
-    @pl.loop(2, last_group)
+    finish(1, 1 - core, 2, wait=False)
+
+    @pl.loop(2, last_group - 1)
     def _(group):
-        finish(group, group_start(group) - core, GROUP)
+        finish(group, group_start(group) - core, GROUP, wait=False)
+
+    finish(last_group - 1, group_start(last_group - 1) - core, GROUP)
 
     pl.when(core == 1)(lambda: finish(last_group, tiles - 2 * SHIFT, 2 * SHIFT))
 

time: 107 us -> 107 us (level)
  no operation moved by 1% of the time
where the time goes in v10:
time: 107 us
  Pallas kernels  107 us (100%)
    pallas_call x1, Pallas kernels, local_head(): pl.pallas_call(functools.partial(head_kernel, sizes), name='head', out_sh...  105 us

profile of v10, /device:TPU:0, one launch (start us, length us, event | category | flops | bytes accessed | tf_op | source)
XLA Modules:
  0.0 107.3 jit_solution(10292147601542298117)
XLA Ops:
  0.6 104.5 %head.1 = (f32[64,16384]{1,0:T(8,128)S(1)}, f32[64,128]{1,0:T(8,128)S(1)}, f32[1,64]{1,0:T(1,128)S(1)}) custom-call(bf16[64,1280]{1,0:T(8,128)(2,1)} %hidden_hbm.1, f32[1280]{0:T(1024)} %gain_hbm.1, bf16[1280,65536]{1,0:T(8,128)(2,1)} %w_hbm.1), custom_call_target="tpu_custom_call" | custom-call | tf_op jit(solution)/shard_map/head/pallas_call | solution.py:415
  105.2 2.1 %subtract.1 = (f32[64,16384]{1,0:T(8,128)}, f32[64]{0:T(128)}) custom-call(f32[64,16384]{1,0:T(8,128)S(1)} %get-tuple-element.5.z_ref, f32[64,128]{1,0:T(8,128)S(1)} %get-tuple-element.6.lse_col_ref, f32[1,64]{1,0:T(1,128)S(1)} %get-tuple-element.7.lse_row_ref), custom_call_target="tpu_custom_call" | custom-call | tf_op jit(solution)/shard_map/subtract/pallas_call | solution.py:464

commit v11 on v9

--- a/solution.py
+++ b/solution.py
@@ -13,7 +13,6 @@
 TILE = 512
 PAIRS = 6
 GROUP = 4
-EARLY = 2
 EDGE = 128
 SHIFT = 1
 SUBLANES = 8
@@ -170,12 +169,8 @@
             w_copy(q, False).start()
             w_copy(q, True).start()
 
-    edge_fetch(0).start()
-    edge_fetch(1).start()
-    fetch(0, EARLY)
 
     h_copy.wait()
-    gain_copy.wait()
     squares = jnp.zeros((batch, LANES), jnp.float32)
     for k in range(width // LANES):
         part = h_ref[:, k * LANES:(k + 1) * LANES].astype(jnp.float32)
@@ -195,9 +190,13 @@
 
     for k in range(rows - 1):
         sq_copy(k).start()
-    fetch(EARLY, PAIRS)
+    edge_fetch(0).start()
+    edge_fetch(1).start()
+    fetch(0, 1)
+    gain_copy.wait()
     for k in reversed(range(rows - 1)):
         sq_copy(k, arrival=True).wait_recv()
+    fetch(1, 2)
     total_sq = sq_in[0]
     for k in range(1, rows):
         total_sq = total_sq + sq_in[k]
@@ -239,11 +238,14 @@
 
     edge_fetch(0).wait()
     edge_fetch(1).wait()
-    edge = jnp.dot(x_ref[...], w_edge[...], preferred_element_type=jnp.float32)
     for k in range(2):
-        edge_out[k] = edge[:, k * EDGE:(k + 1) * EDGE]
+        at = slice(k * EDGE, (k + 1) * EDGE)
+        edge_out[k] = jnp.dot(x_ref[...], w_edge[:, at], preferred_element_type=jnp.float32)
+    for k in range(2):
         edge_copy(k).start()
+    fetch(2, 4)
     partner_tile(0, EDGE)
+    fetch(4, PAIRS)
     partner_tile(1)
     own_tile(0, chip_out.at[0, :, pl.ds(EDGE, TILE - EDGE)], EDGE)
     chip_copy(0, 0, 1, EDGE).start()

time: 107 us -> 107 us (level)
  no operation moved by 1% of the time
where the time goes in v11:
time: 107 us
  Pallas kernels  107 us (100%)
    pallas_call x1, Pallas kernels, local_head(): pl.pallas_call(functools.partial(head_kernel, sizes), name='head', out_sh...  104 us

profile of v11, /device:TPU:0, one launch (start us, length us, event | category | flops | bytes accessed | tf_op | source)
XLA Modules:
  0.0 107.3 jit_solution(7769592422048578161)
XLA Ops:
  0.6 104.5 %head.1 = (f32[64,16384]{1,0:T(8,128)S(1)}, f32[64,128]{1,0:T(8,128)S(1)}, f32[1,64]{1,0:T(1,128)S(1)}) custom-call(bf16[64,1280]{1,0:T(8,128)(2,1)} %hidden_hbm.1, f32[1280]{0:T(1024)} %gain_hbm.1, bf16[1280,65536]{1,0:T(8,128)(2,1)} %w_hbm.1), custom_call_target="tpu_custom_call" | custom-call | tf_op jit(solution)/shard_map/head/pallas_call | solution.py:405
  105.1 2.1 %subtract.1 = (f32[64,16384]{1,0:T(8,128)}, f32[64]{0:T(128)}) custom-call(f32[64,16384]{1,0:T(8,128)S(1)} %get-tuple-element.5.z_ref, f32[64,128]{1,0:T(8,128)S(1)} %get-tuple-element.6.lse_col_ref, f32[1,64]{1,0:T(1,128)S(1)} %get-tuple-element.7.lse_row_ref), custom_call_target="tpu_custom_call" | custom-call | tf_op jit(solution)/shard_map/subtract/pallas_call | solution.py:454

commit v12 on v11

--- a/solution.py
+++ b/solution.py
@@ -170,6 +170,10 @@
             w_copy(q, True).start()
 
 
+    edge_fetch(0).start()
+    edge_fetch(1).start()
+    fetch(0, 1)
+
     h_copy.wait()
     squares = jnp.zeros((batch, LANES), jnp.float32)
     for k in range(width // LANES):
@@ -190,13 +194,10 @@
 
     for k in range(rows - 1):
         sq_copy(k).start()
-    edge_fetch(0).start()
-    edge_fetch(1).start()
-    fetch(0, 1)
+    fetch(1, 2)
     gain_copy.wait()
     for k in reversed(range(rows - 1)):
         sq_copy(k, arrival=True).wait_recv()
-    fetch(1, 2)
     total_sq = sq_in[0]
     for k in range(1, rows):
         total_sq = total_sq + sq_in[k]
@@ -270,10 +271,13 @@
     @pl.loop(tiles - SHIFT, tiles + SHIFT)
     def _(s):
         partner_tile(s + 1)
-        pl.when(core == 1)(lambda: send_tile(s))
+
+        @pl.when(core == 1)
+        def _():
+            send_tile(s)
+            chip_copy(last_group + s - tiles + SHIFT, s, 1).start()
+
         pl.when(core == 0)(lambda: keep_tile(s))
-
-    pl.when(core == 1)(lambda: chip_copy(last_group, tiles - SHIFT, 2 * SHIFT).start())
 
     @pl.loop(tiles + SHIFT, 2 * tiles + SHIFT)
     def _(s):
@@ -316,7 +320,10 @@
     def _(group):
         finish(group, group_start(group) - core, GROUP)
 
-    pl.when(core == 1)(lambda: finish(last_group, tiles - 2 * SHIFT, 2 * SHIFT))
+    @pl.when(core == 1)
+    def _():
+        for k in range(2 * SHIFT):
+            finish(last_group + k, tiles - 2 * SHIFT + k, 1)
 
     peaks_by_lane, mass_by_lane = lane_peak[...].T, lane_mass[...].T
     peak = jnp.max(peaks_by_lane, axis=0, keepdims=True)
@@ -356,7 +363,10 @@
     def _(group):
         chip_copy(group, group_start(group), GROUP).wait_send()
 
-    pl.when(core == 1)(lambda: chip_copy(last_group, tiles - SHIFT, 2 * SHIFT).wait_send())
+    @pl.when(core == 1)
+    def _():
+        for k in range(2 * SHIFT):
+            chip_copy(last_group + k, tiles - SHIFT + k, 1).wait_send()
 
     for k in reversed(range(everyone - 1)):
         mass_copy(k, arrival=True).wait_recv()

time: 107 us -> 107 us (level)
  no operation moved by 1% of the time
where the time goes in v12:
time: 107 us
  Pallas kernels  107 us (100%)
    pallas_call x1, Pallas kernels, local_head(): pl.pallas_call(functools.partial(head_kernel, sizes), name='head', out_sh...  104 us

profile of v12, /device:TPU:0, one launch (start us, length us, event | category | flops | bytes accessed | tf_op | source)
XLA Modules:
  0.0 107.2 jit_solution(644783223204953778)
XLA Ops:
  0.6 104.4 %head.1 = (f32[64,16384]{1,0:T(8,128)S(1)}, f32[64,128]{1,0:T(8,128)S(1)}, f32[1,64]{1,0:T(1,128)S(1)}) custom-call(bf16[64,1280]{1,0:T(8,128)(2,1)} %hidden_hbm.1, f32[1280]{0:T(1024)} %gain_hbm.1, bf16[1280,65536]{1,0:T(8,128)(2,1)} %w_hbm.1), custom_call_target="tpu_custom_call" | custom-call | tf_op jit(solution)/shard_map/head/pallas_call | solution.py:415
  105.1 2.1 %subtract.1 = (f32[64,16384]{1,0:T(8,128)}, f32[64]{0:T(128)}) custom-call(f32[64,16384]{1,0:T(8,128)S(1)} %get-tuple-element.5.z_ref, f32[64,128]{1,0:T(8,128)S(1)} %get-tuple-element.6.lse_col_ref, f32[1,64]{1,0:T(1,128)S(1)} %get-tuple-element.7.lse_row_ref), custom_call_target="tpu_custom_call" | custom-call | tf_op jit(solution)/shard_map/subtract/pallas_call | solution.py:464

commit v13 on v12

--- a/solution.py
+++ b/solution.py
@@ -14,6 +14,7 @@
 PAIRS = 6
 GROUP = 4
 EDGE = 128
+PARTS = 4
 SHIFT = 1
 SUBLANES = 8
 VMEM_LIMIT = 48 * 1024 * 1024
@@ -154,9 +155,13 @@
     last_group = 2 + (tiles - SHIFT - 3) // GROUP
     tail = last_group + 1
 
-    h_copy = pltpu.make_async_copy(hidden_hbm, h_ref, h_sem)
+    h_copies = []
+    for k in range(PARTS):
+        rows_k = pl.ds(k * batch // PARTS, batch // PARTS)
+        h_copies.append(pltpu.make_async_copy(hidden_hbm.at[rows_k], h_ref.at[rows_k], h_sem.at[k]))
     gain_copy = pltpu.make_async_copy(gain_hbm, gain_ref, gain_sem)
-    h_copy.start()
+    for copy in h_copies:
+        copy.start()
     gain_copy.start()
 
     barrier = pltpu.get_barrier_semaphore()
@@ -174,7 +179,8 @@
     edge_fetch(1).start()
     fetch(0, 1)
 
-    h_copy.wait()
+    for copy in h_copies:
+        copy.wait()
     squares = jnp.zeros((batch, LANES), jnp.float32)
     for k in range(width // LANES):
         part = h_ref[:, k * LANES:(k + 1) * LANES].astype(jnp.float32)
@@ -244,9 +250,8 @@
         edge_out[k] = jnp.dot(x_ref[...], w_edge[:, at], preferred_element_type=jnp.float32)
     for k in range(2):
         edge_copy(k).start()
-    fetch(2, 4)
     partner_tile(0, EDGE)
-    fetch(4, PAIRS)
+    fetch(2, PAIRS)
     partner_tile(1)
     own_tile(0, chip_out.at[0, :, pl.ds(EDGE, TILE - EDGE)], EDGE)
     chip_copy(0, 0, 1, EDGE).start()
@@ -444,7 +449,7 @@
                 dma((2,)),
                 dma((2,)),
                 dma((4,)),
-                dma,
+                dma((PARTS,)),
                 dma,
                 dma((PAIRS,)),
                 dma((PAIRS,)),

time: 107 us -> 107 us (level)
  no operation moved by 1% of the time
where the time goes in v13:
time: 107 us
  Pallas kernels  106 us (99%)
    pallas_call x1, Pallas kernels, local_head(): pl.pallas_call(functools.partial(head_kernel, sizes), name='head', out_sh...  104 us

profile of v13, /device:TPU:0, one launch (start us, length us, event | category | flops | bytes accessed | tf_op | source)
XLA Modules:
  0.0 106.8 jit_solution(8986772435654600166)
XLA Ops:
  0.6 104.1 %head.1 = (f32[64,16384]{1,0:T(8,128)S(1)}, f32[64,128]{1,0:T(8,128)S(1)}, f32[1,64]{1,0:T(1,128)S(1)}) custom-call(bf16[64,1280]{1,0:T(8,128)(2,1)} %hidden_hbm.1, f32[1280]{0:T(1024)} %gain_hbm.1, bf16[1280,65536]{1,0:T(8,128)(2,1)} %w_hbm.1), custom_call_target="tpu_custom_call" | custom-call | tf_op jit(solution)/shard_map/head/pallas_call | solution.py:420
  104.7 2.1 %subtract.1 = (f32[64,16384]{1,0:T(8,128)}, f32[64]{0:T(128)}) custom-call(f32[64,16384]{1,0:T(8,128)S(1)} %get-tuple-element.5.z_ref, f32[64,128]{1,0:T(8,128)S(1)} %get-tuple-element.6.lse_col_ref, f32[1,64]{1,0:T(1,128)S(1)} %get-tuple-element.7.lse_row_ref), custom_call_target="tpu_custom_call" | custom-call | tf_op jit(solution)/shard_map/subtract/pallas_call | solution.py:469

commit v14 on v13

--- a/solution.py
+++ b/solution.py
@@ -95,7 +95,7 @@
     own_count = tiles - SHIFT + core * 2 * SHIFT
     partner_count = 2 * tiles - own_count
 
-    def w_copy(s, own):
+    def w_copy(s, own, part=None):
         count = own_count if own else partner_count
         side = core if own else 1 - core
         late = jnp.where(s < count, 0, 1)
@@ -103,9 +103,14 @@
         start = (late * chip + (1 - late) * (1 - chip)) * 2 * block + tile * TILE
         buf, sem = (w_own, w_own_sem) if own else (w_partner, w_partner_sem)
         slot = s % PAIRS
+        at = pl.ds(0, width) if part is None else pl.ds(part * width // PARTS, width // PARTS)
         return pltpu.make_async_copy(
-            w_hbm.at[:, pl.ds(pl.multiple_of(start, TILE), TILE)], buf.at[slot], sem.at[slot]
-        )
+            w_hbm.at[at, pl.ds(pl.multiple_of(start, TILE), TILE)], buf.at[slot, at], sem.at[slot]
+        )
+
+    def w_fetch(s, own):
+        for part in range(PARTS):
+            w_copy(s, own, part).start()
 
     def core_copy(s, cut=0):
         at = pl.ds(cut, TILE - cut)
@@ -171,8 +176,8 @@
     def fetch(first, last):
         @pl.loop(first, last)
         def _(q):
-            w_copy(q, False).start()
-            w_copy(q, True).start()
+            w_fetch(q, False)
+            w_fetch(q, True)
 
 
     edge_fetch(0).start()
@@ -200,7 +205,7 @@
 
     for k in range(rows - 1):
         sq_copy(k).start()
-    fetch(1, 2)
+    fetch(1, 3)
     gain_copy.wait()
     for k in reversed(range(rows - 1)):
         sq_copy(k, arrival=True).wait_recv()
@@ -219,7 +224,7 @@
 
         @pl.when(q + PAIRS < partner_count + tiles)
         def _():
-            w_copy(q + PAIRS, False).start()
+            w_fetch(q + PAIRS, False)
 
         core_copy(q, cut).start()
 
@@ -229,7 +234,7 @@
 
         @pl.when(q + PAIRS < own_count + tiles)
         def _():
-            w_copy(q + PAIRS, True).start()
+            w_fetch(q + PAIRS, True)
 
         core_copy(q, cut).wait_recv()
         total[...] += core_in[q, :, cut:]
@@ -251,7 +256,7 @@
     for k in range(2):
         edge_copy(k).start()
     partner_tile(0, EDGE)
-    fetch(2, PAIRS)
+    fetch(3, PAIRS)
     partner_tile(1)
     own_tile(0, chip_out.at[0, :, pl.ds(EDGE, TILE - EDGE)], EDGE)
     chip_copy(0, 0, 1, EDGE).start()
@@ -396,11 +401,13 @@
     for n in range(batch // SUBLANES):
         at = slice(n * SUBLANES, (n + 1) * SUBLANES)
         lse = lse_col_ref[at]
-        for k in range(0, block, LANES):
-            out_ref[at, k:k + LANES] = z_ref[at, k:k + LANES] - lse
-        rows = pl.ds(n * SUBLANES, SUBLANES)
-        copies.append(pltpu.make_async_copy(out_ref.at[rows], out_hbm.at[rows], sem.at[n]))
-        copies[-1].start()
+        for half in range(2):
+            first = half * block // 2
+            for k in range(first, first + block // 2, LANES):
+                out_ref[at, k:k + LANES] = z_ref[at, k:k + LANES] - lse
+            place = (pl.ds(n * SUBLANES, SUBLANES), pl.ds(first, block // 2))
+            copies.append(pltpu.make_async_copy(out_ref.at[place], out_hbm.at[place], sem.at[2 * n + half]))
+            copies[-1].start()
     for copy in copies:
         copy.wait()
 
@@ -475,7 +482,7 @@
             ),
             in_specs=[vmem] * 3,
             out_specs=[hbm] * 2,
-            scratch_shapes=[pltpu.VMEM((batch, block), f32), pltpu.VMEM((batch,), f32), dma((batch // SUBLANES,)), dma],
+            scratch_shapes=[pltpu.VMEM((batch, block), f32), pltpu.VMEM((batch,), f32), dma((2 * batch // SUBLANES,)), dma],
             compiler_params=pltpu.CompilerParams(vmem_limit_bytes=16 * 1024 * 1024),
         )(z, lse_col, lse_row)
 

time: 107 us -> 107 us (level)
  no operation moved by 1% of the time
where the time goes in v14:
time: 107 us
  Pallas kernels  107 us (100%)
    pallas_call x1, Pallas kernels, local_head(): pl.pallas_call(functools.partial(head_kernel, sizes), name='head', out_sh...  104 us
    pallas_call x1, Pallas kernels, local_head(): pl.pallas_call(subtract_kernel, name='subtract', out_shape=(jax.ShapeDtyp...  2.17 us

profile of v14, /device:TPU:0, one launch (start us, length us, event | category | flops | bytes accessed | tf_op | source)
XLA Modules:
  0.0 107.2 jit_solution(14133432765537916658)
XLA Ops:
  0.6 104.4 %head.1 = (f32[64,16384]{1,0:T(8,128)S(1)}, f32[64,128]{1,0:T(8,128)S(1)}, f32[1,64]{1,0:T(1,128)S(1)}) custom-call(bf16[64,1280]{1,0:T(8,128)(2,1)} %hidden_hbm.1, f32[1280]{0:T(1024)} %gain_hbm.1, bf16[1280,65536]{1,0:T(8,128)(2,1)} %w_hbm.1), custom_call_target="tpu_custom_call" | custom-call | tf_op jit(solution)/shard_map/head/pallas_call | solution.py:427
  105.0 2.2 %subtract.1 = (f32[64,16384]{1,0:T(8,128)}, f32[64]{0:T(128)}) custom-call(f32[64,16384]{1,0:T(8,128)S(1)} %get-tuple-element.5.z_ref, f32[64,128]{1,0:T(8,128)S(1)} %get-tuple-element.6.lse_col_ref, f32[1,64]{1,0:T(1,128)S(1)} %get-tuple-element.7.lse_row_ref), custom_call_target="tpu_custom_call" | custom-call | tf_op jit(solution)/shard_map/subtract/pallas_call | solution.py:476

commit v15 on v13

--- a/solution.py
+++ b/solution.py
@@ -14,7 +14,7 @@
 PAIRS = 6
 GROUP = 4
 EDGE = 128
-PARTS = 4
+PARTS = 8
 SHIFT = 1
 SUBLANES = 8
 VMEM_LIMIT = 48 * 1024 * 1024

time: 107 us -> 107 us (level)
  no operation moved by 1% of the time
where the time goes in v15:
time: 107 us
  Pallas kernels  106 us (99%)
    pallas_call x1, Pallas kernels, local_head(): pl.pallas_call(functools.partial(head_kernel, sizes), name='head', out_sh...  104 us

profile of v15, /device:TPU:0, one launch (start us, length us, event | category | flops | bytes accessed | tf_op | source)
XLA Modules:
  0.0 106.9 jit_solution(10216029837376079454)
XLA Ops:
  0.6 104.1 %head.1 = (f32[64,16384]{1,0:T(8,128)S(1)}, f32[64,128]{1,0:T(8,128)S(1)}, f32[1,64]{1,0:T(1,128)S(1)}) custom-call(bf16[64,1280]{1,0:T(8,128)(2,1)} %hidden_hbm.1, f32[1280]{0:T(1024)} %gain_hbm.1, bf16[1280,65536]{1,0:T(8,128)(2,1)} %w_hbm.1), custom_call_target="tpu_custom_call" | custom-call | tf_op jit(solution)/shard_map/head/pallas_call | solution.py:420
  104.8 2.1 %subtract.1 = (f32[64,16384]{1,0:T(8,128)}, f32[64]{0:T(128)}) custom-call(f32[64,16384]{1,0:T(8,128)S(1)} %get-tuple-element.5.z_ref, f32[64,128]{1,0:T(8,128)S(1)} %get-tuple-element.6.lse_col_ref, f32[1,64]{1,0:T(1,128)S(1)} %get-tuple-element.7.lse_row_ref), custom_call_target="tpu_custom_call" | custom-call | tf_op jit(solution)/shard_map/subtract/pallas_call | solution.py:469
